TPU v7x, 128 devices: a whole 4x4x4 slice. The times are simulated.
128 devices in a mesh: sys: 1, zdom: 2 (over core), ydom: 64 (over z, y, x).
Axes of the slice: x: 4, y: 4, z: 4, core: 2. Of those that a mesh axis runs over, the one named last changes fastest.
Arguments:
- charge: float32 [2097152], P(('sys', 'ydom', 'zdom'))
- real_mask: int32 [2097152], P(('sys', 'ydom', 'zdom'))
- grid_idx: int32 [2097152, 3], P(('sys', 'ydom', 'zdom'))
- spline_w: float32 [2097152, 3, 4], P(('sys', 'ydom', 'zdom'))
- influence: float32 [384, 384, 384], P(('sys', 'ydom'), 'zdom')
Outputs:
- output 1: float32 [384, 384, 384], P(('sys', 'ydom'), 'zdom')
- output 2: float32 [1], P('sys')
All inputs are finite; a program needn't handle non-finite values.
Results may differ from a plain program's by a relative error of at most 0.001.
Values are sent between devices in bfloat16 or wider.
A program may use at most 1 GiB of HBM per device.

v0:
```python
import math
import jax
import jax.numpy as jnp
from jax import lax
from jax.sharding import PartitionSpec as P

PRECISE = lax.Precision.HIGHEST
GHOST_PLANES = 3


def tap_weights(base, taps_w, length):
    position = (base[..., None] + jnp.arange(4)) % length
    hit_mask = jnp.arange(length)[:, None] == position[..., None, :]
    return jnp.sum(jnp.where(hit_mask, taps_w[..., None, :], 0.0), axis=-1)


def spread_block(charge, real_mask, grid_idx, spline_w, grid_n, len_y, len_z):
    weight = charge * real_mask.astype(jnp.float32)
    line_x = tap_weights(grid_idx[..., 0], spline_w[..., 0, :], grid_n) * weight[..., None]
    line_y = tap_weights(grid_idx[..., 1], spline_w[..., 1, :], len_y + GHOST_PLANES)
    line_z = tap_weights(grid_idx[..., 2], spline_w[..., 2, :], len_z + GHOST_PLANES)
    plane_yz = line_y[..., :, None] * line_z[..., None, :]
    return jnp.einsum('...nx,...nyz->...xyz', line_x, plane_yz, precision=PRECISE, preferred_element_type=jnp.float32)


def dft_parts(grid_n, freq_rows):
    phase_idx = (freq_rows[:, None] * jnp.arange(grid_n)[None, :]) % grid_n
    angle_rad = phase_idx.astype(jnp.float32) * (2.0 * math.pi / grid_n)
    return jnp.cos(angle_rad), jnp.sin(angle_rad)


def real_dft(cos_part, sine_part):
    return jnp.stack([cos_part, -sine_part])


def complex_dft(cos_part, sine_part):
    return jnp.stack([jnp.stack([cos_part, sine_part]), jnp.stack([-sine_part, cos_part])])


def fold_ghosts(ext_block, axis_name, axis_size, axis_dim, length):
    ghost_slab = lax.slice_in_dim(ext_block, length, length + GHOST_PLANES, axis=axis_dim)
    recv_slab = lax.ppermute(ghost_slab, axis_name, [(source, (source + 1) % axis_size) for source in range(axis_size)])
    head_planes = lax.slice_in_dim(ext_block, 0, GHOST_PLANES, axis=axis_dim) + recv_slab
    rest_planes = lax.slice_in_dim(ext_block, GHOST_PLANES, length, axis=axis_dim)
    return jnp.concatenate([head_planes, rest_planes], axis=axis_dim)


def solution(mesh):
    y_devs = mesh.shape['ydom']
    z_devs = mesh.shape['zdom']
    slot_spec = P(('sys', 'ydom', 'zdom'))
    mode_spec = P(('sys', 'ydom'), 'zdom', None)

    def local_energy(charge, real_mask, grid_idx, spline_w, influence):
        grid_n = influence.shape[2]
        len_y = grid_n // y_devs
        len_z = grid_n // z_devs
        extended = spread_block(charge, real_mask, grid_idx, spline_w, grid_n, len_y, len_z)
        folded_y = fold_ghosts(extended, 'ydom', y_devs, 1, len_y)
        charge_grid = fold_ghosts(folded_y, 'zdom', z_devs, 2, len_z)
        cos_part, sine_part = dft_parts(grid_n, jnp.arange(grid_n))
        full_dft = complex_dft(cos_part, sine_part)
        stage_x = jnp.einsum('rkx,xyz->rkyz', real_dft(cos_part, sine_part), charge_grid, precision=PRECISE, preferred_element_type=jnp.float32)
        stage_x = lax.all_to_all(stage_x, 'ydom', 1, 2, tiled=True)
        stage_y = jnp.einsum('abky,bxyz->axkz', full_dft, stage_x, precision=PRECISE, preferred_element_type=jnp.float32)
        stage_y = lax.all_to_all(stage_y, 'zdom', 2, 3, tiled=True)
        stage_z = jnp.einsum('abkz,bxyz->axyk', full_dft, stage_y, precision=PRECISE, preferred_element_type=jnp.float32)
        mode_energy = 0.5 * influence * (stage_z[0] * stage_z[0] + stage_z[1] * stage_z[1])
        energy = lax.psum(jnp.sum(mode_energy), ('ydom', 'zdom')) / (grid_n * grid_n * grid_n)
        return mode_energy, jnp.reshape(energy, (1,))

    return jax.shard_map(local_energy, mesh=mesh, in_specs=(slot_spec, slot_spec, P(('sys', 'ydom', 'zdom'), None), P(('sys', 'ydom', 'zdom'), None, None), mode_spec), out_specs=(mode_spec, P('sys')), check_vma=False)
```

profile of v0, /device:TPU:1, one launch (start us, length us, event | category | flops | bytes accessed | tf_op | source)
XLA Modules:
  0.0 547.7 jit_solution(17341661172036465382)
XLA Ops:
  1.8 1.4 fusion.57
  4.1 32.0 %select_reduce_fusion = f32[16384,384]{1,0:T(8,128)} fusion(f32[16384,4]{0,1:T(4,128)S(1)} %get-tuple-element.6, s32[16384,4]{0,1:T(4,128)S(1)} %add_select_fusion.3), kind=kLoop, calls=%fused_computation.2 | loop fusion | flops 69206016 | bytes 25690112 | tf_op jit(solution)/shard_map/reduce_sum | solution.py:14
  36.1 55.8 %select_reduce_fusion.1 = f32[16384,195]{0,1:T(8,128)} fusion(f32[16384,4]{0,1:T(4,128)S(1)} %get-tuple-element.7, s32[16384,4]{0,1:T(4,128)S(1)} %add_select_fusion.1), kind=kLoop, calls=%fused_computation.6 | loop fusion | flops 35143680 | bytes 13303808 | tf_op jit(solution)/shard_map/reduce_sum | solution.py:14
  91.9 1.7 select_reduce_fusion.2
  93.6 201.1 %fusion = f32[384,9,195]{0,2,1:T(8,128)S(1)} fusion(f32[16384,195]{0,1:T(8,128)} %select_reduce_fusion.1, f32[16384,9]{0,1:T(8,128)S(1)} %select_reduce_fusion.2, f32[16384,384]{1,0:T(8,128)} %select_reduce_fusion, f32[16384]{0:T(1024)S(1)} %convert_multiply_fusion), kind=kOutput, calls=%fused_computation | convolution fusion | flops 132533108736 | bytes 41296384 | tf_op jit(solution)/shard_map/...nx,...nyz->...xyz/dot_general | solution.py:23
  294.7 2.3 collective-permute-start
  297.0 27.3 %collective-permute-done = f32[384,3,195]{0,2,1:T(8,128)S(1)} collective-permute-done((f32[384,3,195]{0,2,1:T(8,128)S(1)}, f32[384,3,195]{0,2,1:T(8,128)S(1)}, u32[]{:S(2)}, u32[]{:S(2)}) %collective-permute-start) | collective-permute-done | bytes 898592 | tf_op jit(solution)/shard_map/ppermute | solution.py:42
  324.6 1.8 collective-permute-start.1
  326.4 2.4 fusion.39
  329.8 5.7 %fusion.22 = f32[2,384,6,192]{1,3,2,0:T(8,128)S(1)} fusion(f32[384,3,195]{0,2,1:T(8,128)S(1)} %get-tuple-element.5, f32[384,3,195]{0,2,1:T(8,128)S(1)} %get-tuple-element.4, f32[384,6,3]{0,2,1:T(4,128)S(1)} %maximum_add_fusion, f32[1,384,384]{2,1,0:T(8,128)S(1)} %get-tuple-element.14, f32[1,384,384]{2,1,0:T(8,128)S(1)} %get-tuple-element.15), kind=kOutput, calls=%fused_computation.29 | convolution fusion | flops 4079370240 | bytes 6543360 | tf_op jit(solution)/shard_map/rkx,xyz->rkyz/dot_general | solution.py:63
  335.5 5.5 copy.36
  341.0 6.2 %all-to-all-start = ((f32[2,384,6,192]{3,0,2,1:T(2,128)}), f32[2,384,6,192]{3,0,2,1:T(2,128)}, u32[]{:S(2)}, u32[]{:S(2)}) async-start(f32[2,384,6,192]{3,0,2,1:T(2,128)} %copy.36), calls=%async_computation | async-start | bytes 9437184 | tf_op jit(solution)/shard_map/all_to_all | solution.py:64
  347.2 2.2 fusion.38
  349.5 1.6 fusion.30
  351.1 62.4 %all-to-all-done = f32[2,384,6,192]{3,0,2,1:T(2,128)} async-done(((f32[2,384,6,192]{3,0,2,1:T(2,128)}), f32[2,384,6,192]{3,0,2,1:T(2,128)}, u32[]{:S(2)}, u32[]{:S(2)}) %all-to-all-start) | async-done | bytes 3538976 | tf_op jit(solution)/shard_map/all_to_all | solution.py:64
  413.5 4.1 copy.37
  417.6 22.6 %fusion.11 = f32[2,6,384,192]{2,3,0,1:T(8,128)S(1)} fusion(f32[2,6,384,192,1]{3,0,2,1,4:T(2,128)S(1)} %bitcast.64, f32[1,2,384,384]{3,2,1,0:T(8,128)S(1)} %copy-done.2, f32[1,2,384,384]{3,2,1,0:T(8,128)S(1)} %copy-done), kind=kOutput, calls=%fused_computation.19 | convolution fusion | flops 8154316800 | bytes 9437184 | tf_op jit(solution)/shard_map/abky,bxyz->axkz/dot_general | solution.py:65
  440.2 5.3 copy.39
  445.5 8.4 %all_to_all.36 = f32[2,6,384,192]{3,0,1,2:T(2,128)S(1)} all-to-all(f32[2,6,384,192]{3,0,1,2:T(2,128)} %copy.39), channel_id=1, replica_groups=mesh['sys'=1,'zdom'=2,'ydom'=64] {'zdom'}, dimensions={2} | all-to-all | bytes 7077888 | tf_op jit(solution)/shard_map/all_to_all | solution.py:66
  453.9 5.8 %copy.53 = f32[2,6,2,192,192]{4,2,3,0,1:T(2,128)} copy(f32[2,6,2,192,192]{4,0,1,3,2:T(2,128)S(1)} %bitcast.65) | data formatting | bytes 7077888 | tf_op jit(solution)/shard_map/all_to_all | solution.py:66
  459.7 6.9 %reshape.155 = f32[2,6,192,384,1]{3,2,0,1,4:T(8,128)} reshape(f32[2,6,192,2,192]{4,3,2,0,1:T(2,128)} %bitcast.66) | data formatting | bytes 7077888 | tf_op jit(solution)/shard_map/all_to_all | solution.py:66
  466.7 11.3 %fusion.14 = f32[2,6,192,384]{3,2,0,1:T(8,128)S(1)} fusion(f32[2,6,192,384,1]{3,2,0,1,4:T(8,128)} %reshape.155, f32[1,2,384,384]{3,2,1,0:T(8,128)S(1)} %copy-done.3, f32[1,2,384,384]{3,2,1,0:T(8,128)S(1)} %copy-done.1), kind=kOutput, calls=%fused_computation.20 | convolution fusion | flops 8154316800 | bytes 9437184 | tf_op jit(solution)/shard_map/abkz,bxyz->axyk/dot_general | solution.py:67
  478.1 2.3 fusion.55
  480.3 65.1 %psum.7 = f32[]{:T(128)} all-reduce(f32[]{:T(128)} %get-tuple-element.2), channel_id=1, replica_groups=mesh['sys'=1,'zdom'=2,'ydom'=64] {'ydom','zdom'}, use_global_device_ids=true, to_apply=%region_4.5 | all-reduce | flops 1 | bytes 8 | tf_op jit(solution)/shard_map/psum | solution.py:69
  (32 shorter events, 3.3 us)
Async XLA Ops:
  36.1 57.5 %copy-start.9 = (f32[16384]{0:T(1024)S(1)}, f32[16384]{0:T(1024)}, u32[]{:S(2)}) copy-start(f32[16384]{0:T(1024)} %param.5) | copy-start | bytes 196612
  36.1 57.5 %copy-start.10 = (s32[16384]{0:T(1024)S(1)}, s32[16384]{0:T(1024)}, u32[]{:S(2)}) copy-start(s32[16384]{0:T(1024)} %param.6) | copy-start | bytes 196612
  294.7 29.7 %collective-permute-start = (f32[384,3,195]{0,2,1:T(8,128)S(1)}, f32[384,3,195]{0,2,1:T(8,128)S(1)}, u32[]{:S(2)}, u32[]{:S(2)}) collective-permute-start(f32[384,3,195]{0,2,1:T(8,128)S(1)} %slice.59), channel_id=1, source_target_pairs={{0,1},{1,2},{2,3},{3,4},{4,5},{5,6},{6,7},{7,8},{8,9},{9,10},{10,1... | collective-permute-start | bytes 2695688 | tf_op jit(solution)/shard_map/ppermute | solution.py:42
  324.6 4.2 collective-permute-start.1
  328.8 0.8 copy-start.4
  328.8 1.0 copy-start.6
  341.0 8.5 %copy-start.5 = (f32[1,384,384]{2,1,0:T(8,128)S(1)}, f32[1,384,384]{2,1,0:T(8,128)}, u32[]{:S(2)}) copy-start(f32[1,384,384]{2,1,0:T(8,128)} %copy-done.4) | copy-start | bytes 1769476
  341.0 8.5 %copy-start.7 = (f32[1,384,384]{2,1,0:T(8,128)S(1)}, f32[1,384,384]{2,1,0:T(8,128)}, u32[]{:S(2)}) copy-start(f32[1,384,384]{2,1,0:T(8,128)} %copy-done.6) | copy-start | bytes 1769476
  341.0 72.5 %all-to-all-start = ((f32[2,384,6,192]{3,0,2,1:T(2,128)}), f32[2,384,6,192]{3,0,2,1:T(2,128)}, u32[]{:S(2)}, u32[]{:S(2)}) async-start(f32[2,384,6,192]{3,0,2,1:T(2,128)} %copy.36), calls=%async_computation | async-start | bytes 9437184 | tf_op jit(solution)/shard_map/all_to_all | solution.py:64
  413.5 4.1 copy-start
  413.5 4.1 copy-start.2
  459.7 7.0 %copy-start.1 = (f32[1,2,384,384]{3,2,1,0:T(8,128)S(1)}, f32[1,2,384,384]{3,2,1,0:T(8,128)}, u32[]{:S(2)}) copy-start(f32[1,2,384,384]{3,2,1,0:T(8,128)} %get-tuple-element.9) | copy-start | bytes 3538948
  459.7 7.0 %copy-start.3 = (f32[1,2,384,384]{3,2,1,0:T(8,128)S(1)}, f32[1,2,384,384]{3,2,1,0:T(8,128)}, u32[]{:S(2)}) copy-start(f32[1,2,384,384]{3,2,1,0:T(8,128)} %get-tuple-element.10) | copy-start | bytes 3538948
  466.7 11.4 %copy-start.8 = (f32[6,192,384]{2,1,0:T(8,128)S(1)}, f32[6,192,384]{2,1,0:T(8,128)}, u32[]{:S(2)}) copy-start(f32[6,192,384]{2,1,0:T(8,128)} %param.9) | copy-start | bytes 5308420
where the time goes:
time: 555 us; the launch traced here: 548 us
  matrix products  241 us (43%)
  other arithmetic  99.1 us (18%)
  waiting for transfers between devices  89.8 us (16%)
  blocking collectives  73.5 us (13%)
  local copies, waits for them, and re-layouts  31.2 us (6%)
  starting transfers between devices  10.3 us (2%)
    dot_general x1, matrix products, spread_block(): jnp.einsum('...nx,...nyz->...xyz', line_x, plane_yz, precision=PRECISE, p...  201 us
    reduce_sum x3, other arithmetic, tap_weights(): return jnp.sum(jnp.where(hit_mask, taps_w[..., None, :], 0.0), axis=-1)  89.5 us
    psum x1, blocking collectives, local_energy(): lax.psum(jnp.sum(mode_energy), ('ydom', 'zdom'))  65.1 us
    all_to_all x1, waiting for transfers between devices, local_energy(): stage_x = lax.all_to_all(stage_x, 'ydom', 1, 2, tiled=True)  62.4 us
    ppermute x2, waiting for transfers between devices, fold_ghosts(): lax.ppermute(ghost_slab, axis_name, [(source, (source + 1) % axis_size) f...  27.3 us
    dot_general x1, matrix products, local_energy(): jnp.einsum('abky,bxyz->axkz', full_dft, stage_x, precision=PRECISE, prefe...  22.6 us
    all_to_all x2, local copies, waits for them, and re-layouts, local_energy(): stage_y = lax.all_to_all(stage_y, 'zdom', 2, 3, tiled=True)  12.7 us
    dot_general x1, matrix products, local_energy(): jnp.einsum('abkz,bxyz->axyk', full_dft, stage_y, precision=PRECISE, prefe...  11.3 us
  transfers between devices with their start and end apart: 3, of which 2 were waited for; matrix products, arithmetic and copies ran while one was open for 1% of the time, Pallas kernels for 0%

commit v1 on v0

v1 whole, which is shorter than its diff:
```python
import functools
import jax
import jax.numpy as jnp
import numpy as np
from jax import lax
from jax.experimental import pallas as pl
from jax.experimental.pallas import tpu as pltpu
from jax.sharding import PartitionSpec as P

G = 384
TAPS = 4
NY = 64
LEN_Y = 6
LEN_Z = 192
EXT_Y = 9
CHUNK = 512
LANES = 128
TILES = 14
COLS = TILES * LANES
ROWS = 12
BLOCK = ROWS * TILES
BF = jnp.bfloat16
F32 = jnp.float32

LOW_TILE = 1
HIGH_TILE = 10


def split_np(table):
    high = table.astype(np.float32).astype(jnp.bfloat16)
    low = (table - high.astype(np.float64)).astype(np.float32).astype(jnp.bfloat16)
    return high, low


def twiddles():
    phase = (np.arange(G)[:, None] * np.arange(G)[None, :]) % G
    angle = phase * (2.0 * np.pi / G)
    cos_part, sine_part = np.cos(angle), np.sin(angle)
    freq = (6 * np.arange(NY)[None, :] + np.arange(6)[:, None]).reshape(-1)
    x_rows = np.concatenate([cos_part[freq], -sine_part[freq]], axis=0)
    both = np.concatenate([cos_part, sine_part], axis=1)
    return split_np(x_rows) + split_np(both)


def split(value):
    high = value.astype(BF)
    return high, (value - high.astype(F32)).astype(BF)


def dot(a, b):
    return lax.dot_general(a, b, (((1,), (0,)), ((), ())), preferred_element_type=F32)


def dot_nt(a, b):
    return lax.dot_general(a, b, (((1,), (1,)), ((), ())), preferred_element_type=F32)


def row_iota(first, rows):
    return lax.broadcasted_iota(jnp.int32, (rows, CHUNK), 0) + first


def pick(rows, positions, weights):
    line = jnp.where(rows == positions[3], weights[3], 0.0)
    for s in (2, 1, 0):
        line = jnp.where(rows == positions[s], weights[s], line)
    return line


def spread_kernel(w_ref, idx_ref, q_ref, m_ref, fh_ref, fl_ref, msg_ref, acc_ref, lz_ref, qh_ref, ql_ref, *bufs):
    slots = q_ref.shape[1]

    def build(step, ah, al, bh, bl):
        span = pl.ds(pl.multiple_of(step * CHUNK, CHUNK), CHUNK)
        charge = q_ref[:, span] * m_ref[:, span].astype(F32)

        def rows16(value):
            return jnp.broadcast_to(value, (16, CHUNK))

        def taps(dim, scale, modulus):
            base = idx_ref[dim : dim + 1, span]
            positions, weights = [], []
            for s in range(TAPS):
                position = base + s
                if modulus is not None:
                    position = jnp.where(position >= modulus, position - modulus, position)
                weight = w_ref[dim, s : s + 1, span]
                positions.append(rows16(position))
                weights.append(rows16(weight if scale is None else weight * scale))
            return positions, weights

        pos_x, wgt_x = taps(0, charge, G)
        for g in range(G // 16):
            high, low = split(pick(row_iota(16 * g, 16), pos_x, wgt_x))
            ah[16 * g : 16 * g + 16, :] = high
            al[16 * g : 16 * g + 16, :] = low
        pos_z, wgt_z = taps(2, None, None)
        for g in range(LEN_Z // 16):
            lz_ref[16 * g : 16 * g + 16, :] = pick(row_iota(16 * g, 16), pos_z, wgt_z)
        pos_y, wgt_y = taps(1, None, None)
        for g in range(4):
            rows = row_iota(16 * g, 16)
            value = pick(lax.shift_right_logical(rows, 2), pos_y, wgt_y) * pick(
                LEN_Z + lax.bitwise_and(rows, 3), pos_z, wgt_z
            )
            high, low = split(value)
            bh[64 + 16 * g : 80 + 16 * g, :] = high
            bl[64 + 16 * g : 80 + 16 * g, :] = low
        for y in range(EXT_Y):
            line = pick(jnp.full((16, CHUNK), y, jnp.int32), pos_y, wgt_y)
            for g in range(LEN_Z // 16):
                if g < 8:
                    first = LANES * (LOW_TILE + y) + 16 * g
                elif y == 8:
                    first = 16 * (g - 8)
                else:
                    first = LANES * HIGH_TILE + 64 * y + 16 * (g - 8)
                high, low = split(lz_ref[16 * g : 16 * g + 16, :] * line)
                bh[first : first + 16, :] = high
                bl[first : first + 16, :] = low

    def accumulate(ah, al, bh, bl):
        for t in range(TILES // 2):
            cols = slice(256 * t, 256 * t + 256)
            part = dot_nt(ah[...], bh[cols, :]) + dot_nt(al[...], bh[cols, :]) + dot_nt(ah[...], bl[cols, :])
            acc_ref[:, cols] += part

    first, second = bufs[:4], bufs[4:]
    acc_ref[...] = jnp.zeros_like(acc_ref)
    build(0, *first)
    chunks = slots // CHUNK

    def body(pair, carry):
        accumulate(*first)
        build(2 * pair + 1, *second)
        accumulate(*second)
        build(jnp.minimum(2 * pair + 2, chunks - 1), *first)
        return carry

    lax.fori_loop(0, chunks // 2, body, 0)

    for t in range(TILES // 2):
        cols = slice(256 * t, 256 * t + 256)
        high, low = split(acc_ref[:, cols])
        qh_ref[:, cols] = high
        ql_ref[:, cols] = low
    for t in range(TILES // 2):
        cols = slice(256 * t, 256 * t + 256)
        part = dot(fh_ref[...], qh_ref[:, cols]) + dot(fl_ref[...], qh_ref[:, cols]) + dot(fh_ref[...], ql_ref[:, cols])
        for half in range(2):
            for r in range(ROWS):
                msg_ref[pl.ds((2 * t + half) * ROWS + r, NY, stride=BLOCK), :] = part[
                    NY * r : NY * r + NY, LANES * half : LANES * half + LANES
                ]


def spread(w, idx, charge, mask, fh, fl):
    return pl.pallas_call(
        spread_kernel,
        out_shape=jax.ShapeDtypeStruct((NY * BLOCK, LANES), F32),
        in_specs=[pl.BlockSpec(memory_space=pltpu.VMEM)] * 6,
        out_specs=pl.BlockSpec(memory_space=pltpu.VMEM),
        scratch_shapes=[
            pltpu.VMEM((G, COLS), F32),
            pltpu.VMEM((LEN_Z, CHUNK), F32),
            pltpu.VMEM((G, COLS), BF),
            pltpu.VMEM((G, COLS), BF),
        ]
        + [
            pltpu.VMEM((G, CHUNK), BF),
            pltpu.VMEM((G, CHUNK), BF),
            pltpu.VMEM((COLS, CHUNK), BF),
            pltpu.VMEM((COLS, CHUNK), BF),
        ]
        * 2,
        compiler_params=pltpu.CompilerParams(vmem_limit_bytes=60 * 1024 * 1024),
        name="spread",
    )(w, idx, charge, mask, fh, fl)


def y_kernel(recv_ref, ghost_ref, ch_ref, cl_ref, out_ref, x_ref, rh_ref, rl_ref):
    lane = lax.broadcasted_iota(jnp.int32, (NY, LANES), 1)

    def tile(t, row):
        return recv_ref[pl.ds(t * ROWS + row, NY, stride=BLOCK), :]

    def before(value):
        return pltpu.roll(value, 1, 0)

    def half_turn(value):
        return pltpu.roll(value, 64, 1)

    for pair in range(3):
        for part in range(2):
            high_tiles = []
            for odd in range(2):
                row = 6 * part + 2 * pair + odd
                edge = tile(0, row)
                ghost = ghost_ref[pl.ds(row, NY, stride=16), :]

                def low(y):
                    moved = pltpu.roll(ghost, LANES - 64 - 4 * y, 1)
                    return tile(LOW_TILE + y, row) + jnp.where(lane < 3, moved, 0.0)

                for y in range(LEN_Y):
                    value = low(y)
                    if y < 3:
                        value = value + before(low(y + 6))
                    x_ref[pl.ds(G * odd + y, NY, stride=LEN_Y), :] = value
                tiles = [tile(HIGH_TILE + k, row) for k in range(3)]
                tiles[0] = tiles[0] + before(tile(HIGH_TILE + 3, row))
                tiles[1] = tiles[1] + jnp.where(lane < 64, before(edge), 0.0)
                high_tiles.append(tiles)
            for k in range(3):
                even, odd = high_tiles[0][k], high_tiles[1][k]
                x_ref[pl.ds(2 * G + 2 * k, NY, stride=LEN_Y), :] = jnp.where(lane < 64, even, half_turn(odd))
                x_ref[pl.ds(2 * G + 2 * k + 1, NY, stride=LEN_Y), :] = jnp.where(lane < 64, half_turn(even), odd)
            for k in range(3):
                high, low_part = split(x_ref[G * k : G * k + G, :])
                own = slice(G * part + LANES * k, G * part + LANES * k + LANES)
                rh_ref[0:G, own] = high
                rl_ref[0:G, own] = low_part
                swapped = slice(G * (1 - part) + LANES * k, G * (1 - part) + LANES * k + LANES)
                rh_ref[G : 2 * G, swapped] = high if part else -high
                rl_ref[G : 2 * G, swapped] = low_part if part else -low_part
        for t in range(3):
            cols = slice(256 * t, 256 * t + 256)
            out_ref[pair, :, cols] = (
                dot(ch_ref[...], rh_ref[:, cols]) + dot(cl_ref[...], rh_ref[:, cols]) + dot(ch_ref[...], rl_ref[:, cols])
            )


def y_transform(recv, ghost, ch, cl):
    return pl.pallas_call(
        y_kernel,
        out_shape=jax.ShapeDtypeStruct((3, G, 2 * G), F32),
        in_specs=[pl.BlockSpec(memory_space=pltpu.VMEM)] * 4,
        out_specs=pl.BlockSpec(memory_space=pltpu.VMEM),
        scratch_shapes=[pltpu.VMEM((3 * G, LANES), F32), pltpu.VMEM((2 * G, 2 * G), BF), pltpu.VMEM((2 * G, 2 * G), BF)],
        compiler_params=pltpu.CompilerParams(vmem_limit_bytes=40 * 1024 * 1024),
        name="y_transform",
    )(recv, ghost, ch, cl)


def z_kernel(in_ref, ch_ref, cl_ref, bc_ref, out_ref, sum_ref, rh_ref, rl_ref, lh_ref, ll_ref):
    lane = lax.broadcasted_iota(jnp.int32, (LEN_Z, LANES), 1)
    for src, dst in ((ch_ref, rh_ref), (cl_ref, rl_ref)):

        def place(first, rows, z, part):
            cos_part = src[z : z + rows, 0:G]
            sine_part = src[z : z + rows, G : 2 * G]
            dst[first : first + rows, 0:G] = sine_part if part else cos_part
            dst[first : first + rows, G : 2 * G] = cos_part if part else -sine_part

        for half in range(2):
            for part in range(2):
                place(LANES * (2 * half + part), LANES, LEN_Z * half, part)
                place(512 + LANES * half + 64 * part, 64, LEN_Z * half + LANES, part)
    total = jnp.zeros((8, G), F32)
    for pair in range(3):
        for odd in range(2):
            rows = slice(LEN_Z * odd, LEN_Z * odd + LEN_Z)

            def put(col, value):
                high, low = split(value)
                lh_ref[rows, col : col + LANES] = high
                ll_ref[rows, col : col + LANES] = low

            for half in range(2):
                highs = []
                for part in range(2):
                    first = G * part + LANES * odd
                    put(LANES * (2 * half + part), in_ref[half, pair, :, first : first + LANES])
                    highs.append(in_ref[half, pair, :, G * part + 256 : G * part + 384])
                if odd:
                    merged = jnp.where(lane < 64, pltpu.roll(highs[0], 64, 1), highs[1])
                else:
                    merged = jnp.where(lane < 64, highs[0], pltpu.roll(highs[1], 64, 1))
                put(512 + LANES * half, merged)
        mode = (
            dot(lh_ref[...], rh_ref[...]) + dot(ll_ref[...], rh_ref[...]) + dot(lh_ref[...], rl_ref[...])
        )
        for odd in range(2):
            real = mode[LEN_Z * odd : LEN_Z * odd + LEN_Z, 0:G]
            imag = mode[LEN_Z * odd : LEN_Z * odd + LEN_Z, G : 2 * G]
            value = 0.5 * bc_ref[2 * pair + odd] * (real * real + imag * imag)
            out_ref[2 * pair + odd] = value
            total = total + jnp.sum(value.reshape(LEN_Z // 8, 8, G), axis=0)
    sum_ref[...] = total


def z_transform(halves, ch, cl, influence):
    return pl.pallas_call(
        z_kernel,
        out_shape=(jax.ShapeDtypeStruct((6, LEN_Z, G), F32), jax.ShapeDtypeStruct((8, G), F32)),
        in_specs=[pl.BlockSpec(memory_space=pltpu.VMEM)] * 4,
        out_specs=(pl.BlockSpec(memory_space=pltpu.VMEM),) * 2,
        scratch_shapes=[pltpu.VMEM((2 * G, 2 * G), BF)] * 2 + [pltpu.VMEM((G, 2 * G), BF)] * 2,
        compiler_params=pltpu.CompilerParams(vmem_limit_bytes=40 * 1024 * 1024),
        name="z_transform",
    )(halves, ch, cl, influence)


def solution(mesh):
    slots = ('sys', 'ydom', 'zdom')
    mode_spec = P(('sys', 'ydom'), 'zdom', None)
    tables = twiddles()

    def local_energy(charge, real_mask, grid_idx, spline_w, influence):
        fh, fl, ch, cl = [jnp.asarray(table) for table in tables]
        w = jnp.transpose(spline_w, (1, 2, 0))
        idx = jnp.transpose(grid_idx, (1, 0))
        msg = spread(w, idx, charge[None, :], real_mask[None, :], fh, fl).reshape(NY, BLOCK, LANES)
        ghost = lax.ppermute(msg[:, 0:16, :], 'zdom', [(0, 1), (1, 0)])
        recv = lax.all_to_all(jnp.concatenate([msg, ghost], axis=1), 'ydom', 0, 0, tiled=True)
        ghost = recv[:, BLOCK:, :].reshape(NY * 16, LANES)
        planes = y_transform(recv[:, :BLOCK, :].reshape(NY * BLOCK, LANES), ghost, ch, cl)
        halves = lax.all_to_all(planes.reshape(3, 2, LEN_Z, 2 * G).transpose(1, 0, 2, 3), 'zdom', 0, 0, tiled=True)
        mode_energy, sums = z_transform(halves, ch, cl, influence)
        energy = lax.psum(jnp.sum(sums), ('ydom', 'zdom')) / (G * G * G)
        return mode_energy, jnp.reshape(energy, (1,))

    return jax.shard_map(local_energy, mesh=mesh, in_specs=(P(slots), P(slots), P(slots, None), P(slots, None, None), mode_spec), out_specs=(mode_spec, P('sys')), check_vma=False)
```

time: 555 us -> 281 us (0.51); the launches traced: 548 us -> 280 us
  matrix products: 241 us -> 0 us
  Pallas kernels: 0 us -> 105 us
  other arithmetic: 99.1 us -> 3.55 us
  blocking collectives: 73.5 us -> 164 us
  waiting for transfers between devices: 89.8 us -> 1.54 us
  local copies, waits for them, and re-layouts: 31.2 us -> 2.58 us
  starting transfers between devices: 10.3 us -> 1.44 us
    dot_general x4 -> x0, matrix products: 241 us -> none  [the longest x1 201 us: spread_block(): jnp.einsum('...nx,...nyz->...xyz', line_x, plane_yz, precision=PRECISE, p...]
    pallas_call x0 -> x3, Pallas kernels: none -> 105 us  [the longest x1 93.5 us: spread(): pl.pallas_call(spread_kernel, out_shape=jax.ShapeDtypeStruct((NY * BLOCK,...]
    all_to_all x1 -> x2, blocking collectives: 8.39 us -> 100 us  [the longest x1 91.4 us: local_energy(): lax.all_to_all(jnp.concatenate([msg, ghost], axis=1), 'ydom', 0, 0, tiled...]
    reduce_sum x4 -> x1, other arithmetic: 91.7 us -> 0.6 us  [local_energy(): energy = lax.psum(jnp.sum(sums), ('ydom', 'zdom')) / (G * G * G)]
    all_to_all x1 -> x0, waiting for transfers between devices: 62.4 us -> none  [local_energy(): stage_x = lax.all_to_all(stage_x, 'ydom', 1, 2, tiled=True)]
    ppermute x2 -> x1, waiting for transfers between devices: 27.3 us -> 1.54 us  [local_energy(): ghost = lax.ppermute(msg[:, 0:16, :], 'zdom', [(0, 1), (1, 0)])]
    all_to_all x3 -> x0, local copies, waits for them, and re-layouts: 16.8 us -> none  [the longest x2 12.7 us: local_energy(): stage_y = lax.all_to_all(stage_y, 'zdom', 2, 3, tiled=True)]
    all_to_all x1 -> x0, starting transfers between devices: 6.22 us -> none  [local_energy(): stage_x = lax.all_to_all(stage_x, 'ydom', 1, 2, tiled=True)]
  transfers between devices with their start and end apart: 3 -> 1, of which waited for: 2 -> 1; matrix products, arithmetic and copies ran while one was open for 1% -> 0% of each run, Pallas kernels for 0% -> 0%
where the time goes in v1:
time: 281 us; the launch traced here: 280 us
  blocking collectives  164 us (58%)
  Pallas kernels  105 us (37%)
  other arithmetic  3.55 us (1%)
    pallas_call x1, Pallas kernels, spread(): pl.pallas_call(spread_kernel, out_shape=jax.ShapeDtypeStruct((NY * BLOCK,...  93.5 us
    all_to_all x1, blocking collectives, local_energy(): lax.all_to_all(jnp.concatenate([msg, ghost], axis=1), 'ydom', 0, 0, tiled...  91.4 us
    psum x1, blocking collectives, local_energy(): energy = lax.psum(jnp.sum(sums), ('ydom', 'zdom')) / (G * G * G)  63.6 us
    all_to_all x1, blocking collectives, local_energy(): lax.all_to_all(planes.reshape(3, 2, LEN_Z, 2 * G).transpose(1, 0, 2, 3),...  8.93 us
    pallas_call x1, Pallas kernels, z_transform(): pl.pallas_call(z_kernel, out_shape=(jax.ShapeDtypeStruct((6, LEN_Z, G), F...  6 us
  transfers between devices with their start and end apart: 1, of which 1 were waited for; matrix products, arithmetic and copies ran while one was open for 0% of the time, Pallas kernels for 0%

profile of v1, /device:TPU:1, one launch (start us, length us, event | category | flops | bytes accessed | tf_op | source)
XLA Modules:
  0.0 280.4 jit_solution(2635393861508040045)
XLA Ops:
  0.6 93.5 %spread.1 = f32[10752,128]{1,0:T(8,128)} custom-call(f32[3,4,16384]{2,1,0:T(4,128)} %bitcast.18, s32[3,16384]{1,0:T(4,128)} %bitcast.19, f32[1,16384]{1,0:T(1,128)} %bitcast.20, s32[1,16384]{1,0:T(1,128)} %bitcast.21, bf16[768,384]{1,0:T(8,128)(2,1)} %constant.13.clone.fh_ref, bf16[768,384]{1,0:T(8,128)(2,1)} %constant.14.clone.fl_ref), custom_call_target="tpu_custom_call" | custom-call | tf_op jit(solution)/shard_map/spread/pallas_call | solution.py:157
  94.1 1.1 slice.12
  95.2 1.4 collective-permute-start
  96.6 1.5 collective-permute-done
  98.2 2.9 %pad_maximum_fusion = f32[64,184,128]{2,1,0:T(8,128)S(1)} fusion(f32[64,16,128]{2,1,0:T(8,128)S(1)} %collective-permute-done, f32[64,168,128]{2,1,0:T(8,128)} %bitcast.16), kind=kLoop, calls=%fused_computation | loop fusion | flops 1507328 | bytes 12058624 | tf_op jit(solution)/shard_map/concatenate | solution.py:314
  101.1 91.4 %all_to_all.10 = f32[64,184,128]{2,1,0:T(8,128)S(1)} all-to-all(f32[64,184,128]{2,1,0:T(8,128)S(1)} %pad_maximum_fusion), channel_id=1, replica_groups=mesh['sys'=1,'zdom'=2,'ydom'=64] {'ydom'}, dimensions={0} | all-to-all | bytes 12058624 | tf_op jit(solution)/shard_map/all_to_all | solution.py:314
  192.5 0.0 copy-start
  192.5 0.0 copy-start.1
  192.5 0.4 slice.13
  192.9 0.7 copy-done
  193.6 0.2 copy-done.1
  193.8 5.5 %y_transform.1 = f32[3,384,768]{2,1,0:T(8,128)S(1)} custom-call(f32[10752,128]{1,0:T(8,128)S(1)} %bitcast.12, f32[1024,128]{1,0:T(8,128)S(1)} %bitcast.14, bf16[384,768]{1,0:T(8,128)(2,1)S(1)} %copy-done.1, bf16[384,768]{1,0:T(8,128)(2,1)S(1)} %copy-done), custom_call_target="tpu_custom_call" | custom-call | tf_op jit(solution)/shard_map/y_transform/pallas_call | solution.py:233
  199.2 0.0 copy-start.2
  199.3 0.2 copy.13
  199.5 8.9 %all_to_all.11.in_ref = f32[2,3,192,768]{3,2,1,0:T(8,128)S(1)} all-to-all(f32[2,3,192,768]{3,2,1,0:T(8,128)S(1)} %bitcast.17), channel_id=1, replica_groups=mesh['sys'=1,'zdom'=2,'ydom'=64] {'zdom'}, dimensions={0} | all-to-all | bytes 7077888 | tf_op jit(solution)/shard_map/all_to_all | solution.py:317
  208.4 0.0 copy-done.2
  208.4 6.0 %z_transform.1 = (f32[6,192,384]{2,1,0:T(8,128)}, f32[8,384]{1,0:T(8,128)S(1)}) custom-call(f32[2,3,192,768]{3,2,1,0:T(8,128)S(1)} %all_to_all.11.in_ref, bf16[384,768]{1,0:T(8,128)(2,1)S(1)} %copy-done.1, bf16[384,768]{1,0:T(8,128)(2,1)S(1)} %copy-done, f32[6,192,384]{2,1,0:T(8,128)S(1)} %copy-done.2), custom_call_target="tpu_custom_call" | custom-call | tf_op jit(solution)/shard_map/z_transform/pallas_call | solution.py:292
  214.4 0.6 reduce_sum.9
  215.0 63.6 %psum.7 = f32[]{:T(128)} all-reduce(f32[]{:T(128)} %reduce_sum.9), channel_id=1, replica_groups=mesh['sys'=1,'zdom'=2,'ydom'=64] {'ydom','zdom'}, use_global_device_ids=true, to_apply=%region_1.0 | all-reduce | flops 1 | bytes 8 | tf_op jit(solution)/shard_map/psum | solution.py:319
  (1 shorter events, 0.0 us)
Async XLA Ops:
  95.2 3.0 %collective-permute-start = (f32[64,16,128]{2,1,0:T(8,128)S(1)}, f32[64,16,128]{2,1,0:T(8,128)S(1)}, u32[]{:S(2)}, u32[]{:S(2)}) collective-permute-start(f32[64,16,128]{2,1,0:T(8,128)S(1)} %slice.12), channel_id=1, source_target_pairs={{0,64},{64,0},{1,65},{65,1},{2,66},{66,2},{3,67},{67,3},{4,68},{68... | collective-permute-start | bytes 1572872 | tf_op jit(solution)/shard_map/ppermute | solution.py:313
  192.5 1.1 copy-start
  192.5 1.2 copy-start.1
  199.2 9.2 %copy-start.2 = (f32[6,192,384]{2,1,0:T(8,128)S(1)}, f32[6,192,384]{2,1,0:T(8,128)}, u32[]{:S(2)}) copy-start(f32[6,192,384]{2,1,0:T(8,128)} %bc_ref.1) | copy-start | bytes 5308420

commit v2 on v1

--- a/solution.py
+++ b/solution.py
@@ -21,6 +21,9 @@
 BLOCK = ROWS * TILES
 BF = jnp.bfloat16
 F32 = jnp.float32
+MESH = pl.DeviceIdType.MESH
+FULL_SCALE = 32000.0
+LOG_STEP = float(np.log(2.0) / 64.0)
 
 LOW_TILE = 1
 HIGH_TILE = 10
@@ -47,6 +50,10 @@
     return high, (value - high.astype(F32)).astype(BF)
 
 
+def level_code(largest):
+    return jnp.clip(jnp.ceil(jnp.log(jnp.maximum(largest, 1e-30)) * (1.0 / LOG_STEP)), -8000.0, 8000.0)
+
+
 def dot(a, b):
     return lax.dot_general(a, b, (((1,), (0,)), ((), ())), preferred_element_type=F32)
 
@@ -66,7 +73,7 @@
     return line
 
 
-def spread_kernel(w_ref, idx_ref, q_ref, m_ref, fh_ref, fl_ref, msg_ref, acc_ref, lz_ref, qh_ref, ql_ref, *bufs):
+def spread_kernel(w_ref, idx_ref, q_ref, m_ref, fh_ref, fl_ref, msg_ref, acc_ref, lz_ref, qh_ref, ql_ref, modes_ref, rows_ref, *bufs):
     slots = q_ref.shape[1]
 
     def build(step, ah, al, bh, bl):
@@ -146,17 +153,32 @@
     for t in range(TILES // 2):
         cols = slice(256 * t, 256 * t + 256)
         part = dot(fh_ref[...], qh_ref[:, cols]) + dot(fl_ref[...], qh_ref[:, cols]) + dot(fh_ref[...], ql_ref[:, cols])
-        for half in range(2):
-            for r in range(ROWS):
-                msg_ref[pl.ds((2 * t + half) * ROWS + r, NY, stride=BLOCK), :] = part[
-                    NY * r : NY * r + NY, LANES * half : LANES * half + LANES
-                ]
+        modes_ref[:, cols] = part
+        size = jnp.maximum(jnp.abs(part[:, :LANES]), jnp.abs(part[:, LANES:]))
+        largest = size if t == 0 else jnp.maximum(largest, size)
+    code = level_code(jnp.max(largest, axis=1, keepdims=True))
+    inverse = jnp.exp(code * (-LOG_STEP)) * FULL_SCALE
+    lane = lax.broadcasted_iota(jnp.int32, (ROWS * NY, LANES), 1)
+    for t in range(TILES):
+        value = modes_ref[:, LANES * t : LANES * t + LANES] * inverse
+        if t == 0:
+            value = jnp.where(lane == LANES - 1, code, value)
+        for r in range(ROWS):
+            rows_ref[pl.ds(t * ROWS + r, NY, stride=BLOCK), :] = value[NY * r : NY * r + NY, :]
+
+    def pack(peer, carry):
+        span = pl.ds(pl.multiple_of(peer * BLOCK, 8), BLOCK)
+        value = lax.round(rows_ref[span, :], lax.RoundingMethod.TO_NEAREST_EVEN)
+        msg_ref[peer] = value.astype(jnp.int32).astype(jnp.int16)
+        return carry
+
+    lax.fori_loop(0, NY, pack, 0)
 
 
 def spread(w, idx, charge, mask, fh, fl):
     return pl.pallas_call(
         spread_kernel,
-        out_shape=jax.ShapeDtypeStruct((NY * BLOCK, LANES), F32),
+        out_shape=jax.ShapeDtypeStruct((NY, BLOCK, LANES), jnp.int16),
         in_specs=[pl.BlockSpec(memory_space=pltpu.VMEM)] * 6,
         out_specs=pl.BlockSpec(memory_space=pltpu.VMEM),
         scratch_shapes=[
@@ -164,6 +186,8 @@
             pltpu.VMEM((LEN_Z, CHUNK), F32),
             pltpu.VMEM((G, COLS), BF),
             pltpu.VMEM((G, COLS), BF),
+            pltpu.VMEM((ROWS * NY, COLS), F32),
+            pltpu.VMEM((NY * BLOCK, LANES), F32),
         ]
         + [
             pltpu.VMEM((G, CHUNK), BF),
@@ -177,11 +201,100 @@
     )(w, idx, charge, mask, fh, fl)
 
 
-def y_kernel(recv_ref, ghost_ref, ch_ref, cl_ref, out_ref, x_ref, rh_ref, rl_ref):
+def exchange_kernel(msg_ref, recv_ref, ghost_ref, send_sem, recv_sem, ghost_send_sem, ghost_recv_sem):
+    me, half = lax.axis_index("ydom"), lax.axis_index("zdom")
+    barrier = pltpu.get_barrier_semaphore()
+
+    def greet(peer, carry):
+        for side in range(2):
+            pl.semaphore_signal(barrier, inc=1, device_id={"ydom": peer, "zdom": side}, device_id_type=MESH)
+        return carry
+
+    lax.fori_loop(0, NY, greet, 0)
+    pl.semaphore_wait(barrier, 2 * NY)
+
+    def peer_of(step):
+        shift = lax.rem(step * 23, NY)
+        x = lax.rem(me + shift, 4)
+        y = lax.rem(me // 4 + shift // 4, 4)
+        z = lax.rem(me // 16 + shift // 16, 4)
+        return x + 4 * y + 16 * z
+
+    def send_ghost(step, carry):
+        peer = peer_of(step)
+        pltpu.make_async_remote_copy(
+            src_ref=msg_ref.at[peer, pl.ds(0, 16)],
+            dst_ref=ghost_ref.at[me],
+            send_sem=ghost_send_sem,
+            recv_sem=ghost_recv_sem,
+            device_id={"ydom": peer, "zdom": 1 - half},
+            device_id_type=MESH,
+        ).start()
+        return carry
+
+    def send(step, carry):
+        peer = peer_of(step)
+        pltpu.make_async_remote_copy(
+            src_ref=msg_ref.at[peer],
+            dst_ref=recv_ref.at[me],
+            send_sem=send_sem,
+            recv_sem=recv_sem,
+            device_id={"ydom": peer},
+            device_id_type=MESH,
+        ).start()
+        return carry
+
+    lax.fori_loop(1, NY, send, 0)
+    lax.fori_loop(0, NY, send_ghost, 0)
+    recv_ref[me] = msg_ref[me]
+    others = pl.ds(0, NY - 1)
+    pltpu.make_async_copy(recv_ref.at[others], recv_ref.at[others], recv_sem).wait()
+    pltpu.make_async_copy(ghost_ref, ghost_ref, ghost_recv_sem).wait()
+    pltpu.make_async_copy(recv_ref.at[others], recv_ref.at[others], send_sem).wait()
+    pltpu.make_async_copy(ghost_ref, ghost_ref, ghost_send_sem).wait()
+
+
+def exchange(msg):
+    return pl.pallas_call(
+        exchange_kernel,
+        out_shape=(
+            jax.ShapeDtypeStruct((NY, BLOCK, LANES), jnp.int16),
+            jax.ShapeDtypeStruct((NY, 16, LANES), jnp.int16),
+        ),
+        in_specs=[pl.BlockSpec(memory_space=pltpu.VMEM)],
+        out_specs=(pl.BlockSpec(memory_space=pltpu.VMEM),) * 2,
+        scratch_shapes=[pltpu.SemaphoreType.DMA] * 4,
+        compiler_params=pltpu.CompilerParams(
+            vmem_limit_bytes=16 * 1024 * 1024, collective_id=0, has_side_effects=True
+        ),
+        name="exchange",
+    )(msg)
+
+
+def y_kernel(
+    recv16_ref, ghost16_ref, ch_ref, cl_ref, own_ref, other_ref,
+    recv_ref, ghost_ref, x_ref, rh_ref, rl_ref, away_ref, send_sems, recv_sems,
+):
+    side = lax.axis_index("zdom")
+    barrier = pltpu.get_barrier_semaphore()
+    pl.semaphore_signal(barrier, inc=1, device_id={"zdom": 1 - side}, device_id_type=MESH)
+
+    def unpack(peer, carry):
+        span = pl.ds(pl.multiple_of(peer * BLOCK, 8), BLOCK)
+        recv_ref[span, :] = recv16_ref[peer].astype(jnp.int32).astype(F32)
+        span = pl.ds(pl.multiple_of(peer * 16, 8), 16)
+        ghost_ref[span, :] = ghost16_ref[peer].astype(jnp.int32).astype(F32)
+        return carry
+
+    lax.fori_loop(0, NY, unpack, 0)
+    copies = []
     lane = lax.broadcasted_iota(jnp.int32, (NY, LANES), 1)
 
-    def tile(t, row):
+    def raw(t, row):
         return recv_ref[pl.ds(t * ROWS + row, NY, stride=BLOCK), :]
+
+    def level(coded):
+        return jnp.broadcast_to(jnp.exp(coded[:, LANES - 1 :] * LOG_STEP) * (1.0 / FULL_SCALE), (NY, LANES))
 
     def before(value):
         return pltpu.roll(value, 1, 0)
@@ -194,8 +307,14 @@
             high_tiles = []
             for odd in range(2):
                 row = 6 * part + 2 * pair + odd
-                edge = tile(0, row)
+                edge = raw(0, row)
+                scale = level(edge)
+                edge = edge * scale
                 ghost = ghost_ref[pl.ds(row, NY, stride=16), :]
+                ghost = ghost * level(ghost)
+
+                def tile(t, row):
+                    return raw(t, row) * scale
 
                 def low(y):
                     moved = pltpu.roll(ghost, LANES - 64 - 4 * y, 1)
@@ -224,37 +343,80 @@
                 rl_ref[G : 2 * G, swapped] = low_part if part else -low_part
         for t in range(3):
             cols = slice(256 * t, 256 * t + 256)
-            out_ref[pair, :, cols] = (
+            part = (
                 dot(ch_ref[...], rh_ref[:, cols]) + dot(cl_ref[...], rh_ref[:, cols]) + dot(ch_ref[...], rl_ref[:, cols])
             )
+            upper, lower = part[:LEN_Z], part[LEN_Z:]
+            own_ref[pair, :, cols] = jnp.where(side == 0, upper, lower)
+            away_ref[pair, :, cols] = jnp.where(side == 0, lower, upper)
+        if pair == 0:
+            pl.semaphore_wait(barrier, 1)
+        copies.append(
+            pltpu.make_async_remote_copy(
+                src_ref=away_ref.at[pair],
+                dst_ref=other_ref.at[pair],
+                send_sem=send_sems.at[pair],
+                recv_sem=recv_sems.at[pair],
+                device_id={"zdom": 1 - side},
+                device_id_type=MESH,
+            )
+        )
+        copies[-1].start()
+    for copy in copies:
+        copy.wait()
 
 
 def y_transform(recv, ghost, ch, cl):
+    half = jax.ShapeDtypeStruct((3, LEN_Z, 2 * G), F32)
     return pl.pallas_call(
         y_kernel,
-        out_shape=jax.ShapeDtypeStruct((3, G, 2 * G), F32),
+        out_shape=(half, half),
         in_specs=[pl.BlockSpec(memory_space=pltpu.VMEM)] * 4,
-        out_specs=pl.BlockSpec(memory_space=pltpu.VMEM),
-        scratch_shapes=[pltpu.VMEM((3 * G, LANES), F32), pltpu.VMEM((2 * G, 2 * G), BF), pltpu.VMEM((2 * G, 2 * G), BF)],
-        compiler_params=pltpu.CompilerParams(vmem_limit_bytes=40 * 1024 * 1024),
+        out_specs=(pl.BlockSpec(memory_space=pltpu.VMEM),) * 2,
+        scratch_shapes=[
+            pltpu.VMEM((NY * BLOCK, LANES), F32),
+            pltpu.VMEM((NY * 16, LANES), F32),
+            pltpu.VMEM((3 * G, LANES), F32),
+            pltpu.VMEM((2 * G, 2 * G), BF),
+            pltpu.VMEM((2 * G, 2 * G), BF),
+            pltpu.VMEM((3, LEN_Z, 2 * G), F32),
+            pltpu.SemaphoreType.DMA((3,)),
+            pltpu.SemaphoreType.DMA((3,)),
+        ],
+        compiler_params=pltpu.CompilerParams(
+            vmem_limit_bytes=40 * 1024 * 1024, collective_id=1, has_side_effects=True
+        ),
         name="y_transform",
     )(recv, ghost, ch, cl)
 
 
-def z_kernel(in_ref, ch_ref, cl_ref, bc_ref, out_ref, sum_ref, rh_ref, rl_ref, lh_ref, ll_ref):
+def z_kernel(
+    own_ref, other_ref, ch_ref, cl_ref, bc_ref, out_ref, sum_ref,
+    rh_ref, rl_ref, lh_ref, ll_ref, part_ref, parts_ref, pair_ref, sems,
+):
+    me, side = lax.axis_index("ydom"), lax.axis_index("zdom")
+    barrier = pltpu.get_barrier_semaphore()
+
+    def greet(step, carry):
+        pl.semaphore_signal(barrier, inc=1, device_id={"ydom": lax.rem(me + step, NY)}, device_id_type=MESH)
+        return carry
+
+    lax.fori_loop(1, NY, greet, 0)
+    pl.semaphore_signal(barrier, inc=1, device_id={"zdom": 1 - side}, device_id_type=MESH)
     lane = lax.broadcasted_iota(jnp.int32, (LEN_Z, LANES), 1)
     for src, dst in ((ch_ref, rh_ref), (cl_ref, rl_ref)):
 
-        def place(first, rows, z, part):
-            cos_part = src[z : z + rows, 0:G]
-            sine_part = src[z : z + rows, G : 2 * G]
+        def place(first, rows, half, z, part):
+            span = pl.ds(pl.multiple_of(LEN_Z * (side if half == 0 else 1 - side) + z, 64), rows)
+            cos_part = src[span, 0:G]
+            sine_part = src[span, G : 2 * G]
             dst[first : first + rows, 0:G] = sine_part if part else cos_part
             dst[first : first + rows, G : 2 * G] = cos_part if part else -sine_part
 
         for half in range(2):
             for part in range(2):
-                place(LANES * (2 * half + part), LANES, LEN_Z * half, part)
-                place(512 + LANES * half + 64 * part, 64, LEN_Z * half + LANES, part)
+                place(LANES * (2 * half + part), LANES, half, 0, part)
+                place(512 + LANES * half + 64 * part, 64, half, LANES, part)
     total = jnp.zeros((8, G), F32)
     for pair in range(3):
         for odd in range(2):
@@ -265,12 +427,12 @@
                 lh_ref[rows, col : col + LANES] = high
                 ll_ref[rows, col : col + LANES] = low
 
-            for half in range(2):
+            for half, in_ref in enumerate((own_ref, other_ref)):
                 highs = []
                 for part in range(2):
                     first = G * part + LANES * odd
-                    put(LANES * (2 * half + part), in_ref[half, pair, :, first : first + LANES])
-                    highs.append(in_ref[half, pair, :, G * part + 256 : G * part + 384])
+                    put(LANES * (2 * half + part), in_ref[pair, :, first : first + LANES])
+                    highs.append(in_ref[pair, :, G * part + 256 : G * part + 384])
                 if odd:
                     merged = jnp.where(lane < 64, pltpu.roll(highs[0], 64, 1), highs[1])
                 else:
@@ -285,19 +447,60 @@
             value = 0.5 * bc_ref[2 * pair + odd] * (real * real + imag * imag)
             out_ref[2 * pair + odd] = value
             total = total + jnp.sum(value.reshape(LEN_Z // 8, 8, G), axis=0)
-    sum_ref[...] = total
-
-
-def z_transform(halves, ch, cl, influence):
+    lanes = total[:, :LANES] + total[:, LANES : 2 * LANES] + total[:, 2 * LANES :]
+    part_ref[...] = jnp.sum(lanes, axis=0, keepdims=True)
+    pl.semaphore_wait(barrier, NY)
+
+    def send(step, carry):
+        pltpu.make_async_remote_copy(
+            src_ref=part_ref,
+            dst_ref=parts_ref.at[me],
+            send_sem=sems.at[0],
+            recv_sem=sems.at[1],
+            device_id={"ydom": lax.rem(me + step, NY)},
+            device_id_type=MESH,
+        ).start()
+        return carry
+
+    lax.fori_loop(1, NY, send, 0)
+    parts_ref[me] = part_ref[...]
+    others = pl.ds(0, NY - 1)
+    pltpu.make_async_copy(parts_ref.at[others], parts_ref.at[others], sems.at[1]).wait()
+    pltpu.make_async_copy(parts_ref.at[others], parts_ref.at[others], sems.at[0]).wait()
+    pair_ref[0] = jnp.sum(parts_ref[...], axis=0)
+    copy = pltpu.make_async_remote_copy(
+        src_ref=pair_ref.at[0],
+        dst_ref=pair_ref.at[1],
+        send_sem=sems.at[2],
+        recv_sem=sems.at[3],
+        device_id={"zdom": 1 - side},
+        device_id_type=MESH,
+    )
+    copy.start()
+    copy.wait()
+    energy = jnp.sum(pair_ref[0] + pair_ref[1], axis=1, keepdims=True) * (1.0 / (G * G * G))
+    sum_ref[...] = jnp.broadcast_to(energy, (1, LANES))
+
+
+def z_transform(own, other, ch, cl, influence):
     return pl.pallas_call(
         z_kernel,
-        out_shape=(jax.ShapeDtypeStruct((6, LEN_Z, G), F32), jax.ShapeDtypeStruct((8, G), F32)),
-        in_specs=[pl.BlockSpec(memory_space=pltpu.VMEM)] * 4,
+        out_shape=(jax.ShapeDtypeStruct((6, LEN_Z, G), F32), jax.ShapeDtypeStruct((1, LANES), F32)),
+        in_specs=[pl.BlockSpec(memory_space=pltpu.VMEM)] * 5,
         out_specs=(pl.BlockSpec(memory_space=pltpu.VMEM),) * 2,
-        scratch_shapes=[pltpu.VMEM((2 * G, 2 * G), BF)] * 2 + [pltpu.VMEM((G, 2 * G), BF)] * 2,
-        compiler_params=pltpu.CompilerParams(vmem_limit_bytes=40 * 1024 * 1024),
+        scratch_shapes=[pltpu.VMEM((2 * G, 2 * G), BF)] * 2
+        + [pltpu.VMEM((G, 2 * G), BF)] * 2
+        + [
+            pltpu.VMEM((1, LANES), F32),
+            pltpu.VMEM((NY, 1, LANES), F32),
+            pltpu.VMEM((2, 1, LANES), F32),
+            pltpu.SemaphoreType.DMA((4,)),
+        ],
+        compiler_params=pltpu.CompilerParams(
+            vmem_limit_bytes=40 * 1024 * 1024, collective_id=2, has_side_effects=True
+        ),
         name="z_transform",
-    )(halves, ch, cl, influence)
+    )(own, other, ch, cl, influence)
 
 
 def solution(mesh):
@@ -309,14 +512,10 @@
         fh, fl, ch, cl = [jnp.asarray(table) for table in tables]
         w = jnp.transpose(spline_w, (1, 2, 0))
         idx = jnp.transpose(grid_idx, (1, 0))
-        msg = spread(w, idx, charge[None, :], real_mask[None, :], fh, fl).reshape(NY, BLOCK, LANES)
-        ghost = lax.ppermute(msg[:, 0:16, :], 'zdom', [(0, 1), (1, 0)])
-        recv = lax.all_to_all(jnp.concatenate([msg, ghost], axis=1), 'ydom', 0, 0, tiled=True)
-        ghost = recv[:, BLOCK:, :].reshape(NY * 16, LANES)
-        planes = y_transform(recv[:, :BLOCK, :].reshape(NY * BLOCK, LANES), ghost, ch, cl)
-        halves = lax.all_to_all(planes.reshape(3, 2, LEN_Z, 2 * G).transpose(1, 0, 2, 3), 'zdom', 0, 0, tiled=True)
-        mode_energy, sums = z_transform(halves, ch, cl, influence)
-        energy = lax.psum(jnp.sum(sums), ('ydom', 'zdom')) / (G * G * G)
-        return mode_energy, jnp.reshape(energy, (1,))
+        msg = spread(w, idx, charge[None, :], real_mask[None, :], fh, fl)
+        recv, ghost = exchange(msg)
+        own, other = y_transform(recv, ghost, ch, cl)
+        mode_energy, energy = z_transform(own, other, ch, cl, influence)
+        return mode_energy, energy[0, :1]
 
     return jax.shard_map(local_energy, mesh=mesh, in_specs=(P(slots), P(slots), P(slots, None), P(slots, None, None), mode_spec), out_specs=(mode_spec, P('sys')), check_vma=False)

time: 281 us -> 178 us (0.63)
  blocking collectives: 164 us -> 0 us
  Pallas kernels: 105 us -> 173 us
  other arithmetic: 3.55 us -> 0 us
    all_to_all x2 -> x0, blocking collectives: 100 us -> none  [the longest x1 91.4 us: local_energy(): lax.all_to_all(jnp.concatenate([msg, ghost], axis=1), 'ydom', 0, 0, tiled...]
    psum x1 -> x0, blocking collectives: 63.6 us -> none  [local_energy(): energy = lax.psum(jnp.sum(sums), ('ydom', 'zdom')) / (G * G * G)]
    pallas_call x2 -> x3, Pallas kernels: 98.9 us -> 161 us  [the longest x1 94.4 us: spread(): pl.pallas_call(spread_kernel, out_shape=jax.ShapeDtypeStruct((NY, BLOCK,...]
    pallas_call x1, Pallas kernels: 6 us -> 12 us  [z_transform(): pl.pallas_call(z_kernel, out_shape=(jax.ShapeDtypeStruct((6, LEN_Z, G), F...]
    concatenate x1 -> x0, other arithmetic: 2.95 us -> none  [local_energy(): jnp.concatenate([msg, ghost], axis=1)]
  transfers between devices with their start and end apart: 1 -> 0, of which waited for: 1 -> 0; matrix products, arithmetic and copies ran while one was open for 0% -> 0% of each run, Pallas kernels for 0% -> 0%
where the time goes in v2:
time: 178 us
  Pallas kernels  173 us (97%)
  local copies, waits for them, and re-layouts  3 us (2%)
  between operations  1.85 us (1%)
    pallas_call x1, Pallas kernels, spread(): pl.pallas_call(spread_kernel, out_shape=jax.ShapeDtypeStruct((NY, BLOCK,...  94.4 us
    pallas_call x1, Pallas kernels, exchange(): pl.pallas_call(exchange_kernel, out_shape=(jax.ShapeDtypeStruct((NY, BLOC...  56.7 us
    pallas_call x1, Pallas kernels, z_transform(): pl.pallas_call(z_kernel, out_shape=(jax.ShapeDtypeStruct((6, LEN_Z, G), F...  12 us
    pallas_call x1, Pallas kernels, y_transform(): pl.pallas_call(y_kernel, out_shape=(half, half), in_specs=[pl.BlockSpec(m...  10.2 us

profile of v2, /device:TPU:1, one launch (start us, length us, event | category | flops | bytes accessed | tf_op | source)
XLA Modules:
  0.0 178.2 jit_solution(11678771544880845332)
XLA Ops:
  0.6 94.4 %spread.1.msg_ref = s16[64,168,128]{2,1,0:T(8,128)(2,1)} custom-call(f32[3,4,16384]{2,1,0:T(4,128)} %bitcast.7, s32[3,16384]{1,0:T(4,128)} %bitcast.8, f32[1,16384]{1,0:T(1,128)} %bitcast.9, s32[1,16384]{1,0:T(1,128)} %bitcast.10, bf16[768,384]{1,0:T(8,128)(2,1)} %constant.8.clone.fh_ref, bf16[768,384]{1,0:T(8,128)(2,1)} %constant.9.clone.fl_ref), custom_call_target="tpu_custom_call" | custom-call | tf_op jit(solution)/shard_map/spread/pallas_call | solution.py:179
  95.0 0.0 copy-start
  95.0 1.8 copy-done
  96.8 0.0 copy-start.1
  96.8 0.0 copy-start.2
  96.8 56.7 %exchange.1 = (s16[64,168,128]{2,1,0:T(8,128)(2,1)S(1)}, s16[64,16,128]{2,1,0:T(8,128)(2,1)S(1)}) custom-call(s16[64,168,128]{2,1,0:T(8,128)(2,1)S(1)} %copy-done), custom_call_target="tpu_custom_call" | custom-call | tf_op jit(solution)/shard_map/exchange/pallas_call | solution.py:258
  153.5 0.0 copy-done.1
  153.5 0.0 copy-done.2
  153.5 0.0 copy-start.3
  153.5 10.2 %y_transform.1 = (f32[3,192,768]{2,1,0:T(8,128)S(1)}, f32[3,192,768]{2,1,0:T(8,128)S(1)}) custom-call(s16[64,168,128]{2,1,0:T(8,128)(2,1)S(1)} %get-tuple-element.8.recv16_ref, s16[64,16,128]{2,1,0:T(8,128)(2,1)S(1)} %get-tuple-element.9.ghost16_ref, bf16[384,768]{1,0:T(8,128)(2,1)S(1)} %copy-done.2, bf16[384,768]{1,0:T(8,128)(2,1)S(1)} %copy-done.1), custom_call_target="tpu_custom_call" | custom-call | tf_op jit(solution)/shard_map/y_transform/pallas_call | solution.py:371
  163.8 0.0 copy-done.3
  163.8 12.0 %z_transform.1 = (f32[6,192,384]{2,1,0:T(8,128)S(1)}, f32[1,128]{1,0:T(1,128)S(1)}) custom-call(f32[3,192,768]{2,1,0:T(8,128)S(1)} %get-tuple-element.10.own_ref, f32[3,192,768]{2,1,0:T(8,128)S(1)} %get-tuple-element.11.other_ref, bf16[384,768]{1,0:T(8,128)(2,1)S(1)} %copy-done.2, bf16[384,768]{1,0:T(8,128)(2,1)S(1)} %copy-done.1, f32[6,192,384]{2,1,0:T(8,128)S(1)} %copy-done.3), custom_call_target="tpu_custom_call" | custom-call | tf_op jit(solution)/shard_map/z_transform/pallas_call | solution.py:486
  175.8 1.2 copy.13
Async XLA Ops:
  95.0 1.8 copy-start
  96.8 56.7 %copy-start.1 = (bf16[384,768]{1,0:T(8,128)(2,1)S(1)}, bf16[384,768]{1,0:T(8,128)(2,1)}, u32[]{:S(2)}) copy-start(bf16[384,768]{1,0:T(8,128)(2,1)} %constant.11.clone.cl_ref) | copy-start | bytes 1769476
  96.8 56.7 %copy-start.2 = (bf16[384,768]{1,0:T(8,128)(2,1)S(1)}, bf16[384,768]{1,0:T(8,128)(2,1)}, u32[]{:S(2)}) copy-start(bf16[384,768]{1,0:T(8,128)(2,1)} %constant.10.clone.ch_ref) | copy-start | bytes 1769476
  153.5 10.3 %copy-start.3 = (f32[6,192,384]{2,1,0:T(8,128)S(1)}, f32[6,192,384]{2,1,0:T(8,128)}, u32[]{:S(2)}) copy-start(f32[6,192,384]{2,1,0:T(8,128)} %bc_ref.1) | copy-start | bytes 5308420

commit v3 on v2

--- a/solution.py
+++ b/solution.py
@@ -13,7 +13,9 @@
 LEN_Y = 6
 LEN_Z = 192
 EXT_Y = 9
-CHUNK = 512
+CHUNK = 256
+WINDOW = 128
+X_ROWS = 520
 LANES = 128
 TILES = 14
 COLS = TILES * LANES
@@ -73,37 +75,67 @@
     return line
 
 
-def spread_kernel(w_ref, idx_ref, q_ref, m_ref, fh_ref, fl_ref, msg_ref, acc_ref, lz_ref, qh_ref, ql_ref, modes_ref, rows_ref, *bufs):
-    slots = q_ref.shape[1]
-
-    def build(step, ah, al, bh, bl):
-        span = pl.ds(pl.multiple_of(step * CHUNK, CHUNK), CHUNK)
-        charge = q_ref[:, span] * m_ref[:, span].astype(F32)
-
-        def rows16(value):
-            return jnp.broadcast_to(value, (16, CHUNK))
-
-        def taps(dim, scale, modulus):
-            base = idx_ref[dim : dim + 1, span]
-            positions, weights = [], []
-            for s in range(TAPS):
-                position = base + s
-                if modulus is not None:
-                    position = jnp.where(position >= modulus, position - modulus, position)
-                weight = w_ref[dim, s : s + 1, span]
-                positions.append(rows16(position))
-                weights.append(rows16(weight if scale is None else weight * scale))
-            return positions, weights
-
-        pos_x, wgt_x = taps(0, charge, G)
-        for g in range(G // 16):
+def sort_lanes(key):
+    lane = lax.broadcasted_iota(jnp.int32, key.shape, 1)
+    size = 2
+    while size <= LANES:
+        distance = size // 2
+        while distance:
+            lower = lax.bitwise_and(lane, distance) == 0
+            other = jnp.where(lower, pltpu.roll(key, LANES - distance, 1), pltpu.roll(key, distance, 1))
+            ascending = lax.bitwise_and(lane, size) == 0
+            key = jnp.where(lower == ascending, jnp.minimum(key, other), jnp.maximum(key, other))
+            distance //= 2
+        size *= 2
+    return key
+
+
+def spread_kernel(
+    w_ref, idx_ref, q_ref, m_ref, fh_ref, fl_ref, msg_ref,
+    acc_ref, lz_ref, qh_ref, ql_ref, modes_ref, rows_ref, wgt_ref, base_ref, spare_ref, *bufs,
+):
+    lane = lax.broadcasted_iota(jnp.int32, (LANES, LANES), 1)
+    key = sort_lanes((idx_ref[0] * LANES + lane).astype(F32)).astype(jnp.int32)
+    order = lax.bitwise_and(key, LANES - 1)
+
+    def place(value):
+        return jnp.transpose(jnp.take_along_axis(value, order, axis=1))
+
+    base_ref[0] = jnp.transpose(lax.shift_right_logical(key, 7))
+    base_ref[1] = place(idx_ref[1])
+    base_ref[2] = place(idx_ref[2])
+    charge = q_ref[...] * m_ref[...].astype(F32)
+    for dim in range(3):
+        for s in range(TAPS):
+            value = w_ref[TAPS * dim + s]
+            wgt_ref[TAPS * dim + s] = place(value * charge if dim == 0 else value)
+
+    def row_of(ref, field, step):
+        pieces = [
+            jnp.broadcast_to(ref[field, pl.ds(2 * step + k, 1), :], (16, LANES)) for k in range(2)
+        ]
+        return jnp.concatenate(pieces, axis=1)
+
+    def taps(dim, step, first):
+        base = row_of(base_ref, dim, step) - first
+        return [base + s for s in range(TAPS)], [row_of(wgt_ref, TAPS * dim + s, step) for s in range(TAPS)]
+
+    def build_x(step, first, a):
+        pos_x, wgt_x = taps(0, step, first)
+        for g in range(WINDOW // 16):
             high, low = split(pick(row_iota(16 * g, 16), pos_x, wgt_x))
-            ah[16 * g : 16 * g + 16, :] = high
-            al[16 * g : 16 * g + 16, :] = low
-        pos_z, wgt_z = taps(2, None, None)
+            a[16 * g : 16 * g + 16, :] = high
+            a[WINDOW + 16 * g : WINDOW + 16 * g + 16, :] = low
+
+    def build(step, a, bh, bl):
+        bases = base_ref[0, pl.ds(2 * step, 2), :]
+        first = jnp.min(bases) // 8 * 8
+        windows = (jnp.max(bases) + 3 - first) // WINDOW + 1
+        build_x(step, first, a)
+        pos_z, wgt_z = taps(2, step, 0)
         for g in range(LEN_Z // 16):
             lz_ref[16 * g : 16 * g + 16, :] = pick(row_iota(16 * g, 16), pos_z, wgt_z)
-        pos_y, wgt_y = taps(1, None, None)
+        pos_y, wgt_y = taps(1, step, 0)
         for g in range(4):
             rows = row_iota(16 * g, 16)
             value = pick(lax.shift_right_logical(rows, 2), pos_y, wgt_y) * pick(
@@ -116,38 +148,51 @@
             line = pick(jnp.full((16, CHUNK), y, jnp.int32), pos_y, wgt_y)
             for g in range(LEN_Z // 16):
                 if g < 8:
-                    first = LANES * (LOW_TILE + y) + 16 * g
+                    row = LANES * (LOW_TILE + y) + 16 * g
                 elif y == 8:
-                    first = 16 * (g - 8)
+                    row = 16 * (g - 8)
                 else:
-                    first = LANES * HIGH_TILE + 64 * y + 16 * (g - 8)
+                    row = LANES * HIGH_TILE + 64 * y + 16 * (g - 8)
                 high, low = split(lz_ref[16 * g : 16 * g + 16, :] * line)
-                bh[first : first + 16, :] = high
-                bl[first : first + 16, :] = low
-
-    def accumulate(ah, al, bh, bl):
+                bh[row : row + 16, :] = high
+                bl[row : row + 16, :] = low
+        return first, windows
+
+    def accumulate(first, a, bh, bl):
+        span = pl.ds(pl.multiple_of(first, 8), WINDOW)
         for t in range(TILES // 2):
             cols = slice(256 * t, 256 * t + 256)
-            part = dot_nt(ah[...], bh[cols, :]) + dot_nt(al[...], bh[cols, :]) + dot_nt(ah[...], bl[cols, :])
-            acc_ref[:, cols] += part
-
-    first, second = bufs[:4], bufs[4:]
+            both = dot_nt(a[...], bh[cols, :])
+            acc_ref[span, cols] += both[:WINDOW] + both[WINDOW:] + dot_nt(a[:WINDOW, :], bl[cols, :])
+
+    def remaining(step, first, windows, a, bh, bl):
+        def window(k, carry):
+            build_x(step, first + WINDOW * k, spare_ref)
+            accumulate(first + WINDOW * k, spare_ref, bh, bl)
+            return carry
+
+        lax.fori_loop(1, windows, window, 0)
+
+    one, two = bufs[:3], bufs[3:]
     acc_ref[...] = jnp.zeros_like(acc_ref)
-    build(0, *first)
-    chunks = slots // CHUNK
+    chunks = LANES * LANES // CHUNK
 
     def body(pair, carry):
-        accumulate(*first)
-        build(2 * pair + 1, *second)
-        accumulate(*second)
-        build(jnp.minimum(2 * pair + 2, chunks - 1), *first)
-        return carry
-
-    lax.fori_loop(0, chunks // 2, body, 0)
+        first, windows = carry
+        accumulate(first, *one)
+        next_first, next_windows = build(2 * pair + 1, *two)
+        remaining(2 * pair, first, windows, *one)
+        accumulate(next_first, *two)
+        carry = build(jnp.minimum(2 * pair + 2, chunks - 1), *one)
+        remaining(2 * pair + 1, next_first, next_windows, *two)
+        return carry
+
+    lax.fori_loop(0, chunks // 2, body, build(0, *one))
+    acc_ref[0:8, :] += acc_ref[G : G + 8, :]
 
     for t in range(TILES // 2):
         cols = slice(256 * t, 256 * t + 256)
-        high, low = split(acc_ref[:, cols])
+        high, low = split(acc_ref[:G, cols])
         qh_ref[:, cols] = high
         ql_ref[:, cols] = low
     for t in range(TILES // 2):
@@ -182,7 +227,7 @@
         in_specs=[pl.BlockSpec(memory_space=pltpu.VMEM)] * 6,
         out_specs=pl.BlockSpec(memory_space=pltpu.VMEM),
         scratch_shapes=[
-            pltpu.VMEM((G, COLS), F32),
+            pltpu.VMEM((X_ROWS, COLS), F32),
             pltpu.VMEM((LEN_Z, CHUNK), F32),
             pltpu.VMEM((G, COLS), BF),
             pltpu.VMEM((G, COLS), BF),
@@ -190,8 +235,12 @@
             pltpu.VMEM((NY * BLOCK, LANES), F32),
         ]
         + [
-            pltpu.VMEM((G, CHUNK), BF),
-            pltpu.VMEM((G, CHUNK), BF),
+            pltpu.VMEM((3 * TAPS, LANES, LANES), F32),
+            pltpu.VMEM((3, LANES, LANES), jnp.int32),
+            pltpu.VMEM((2 * WINDOW, CHUNK), BF),
+        ]
+        + [
+            pltpu.VMEM((2 * WINDOW, CHUNK), BF),
             pltpu.VMEM((COLS, CHUNK), BF),
             pltpu.VMEM((COLS, CHUNK), BF),
         ]
@@ -510,9 +559,10 @@
 
     def local_energy(charge, real_mask, grid_idx, spline_w, influence):
         fh, fl, ch, cl = [jnp.asarray(table) for table in tables]
-        w = jnp.transpose(spline_w, (1, 2, 0))
-        idx = jnp.transpose(grid_idx, (1, 0))
-        msg = spread(w, idx, charge[None, :], real_mask[None, :], fh, fl)
+        square = (LANES, LANES)
+        w = jnp.transpose(spline_w, (1, 2, 0)).reshape(3 * TAPS, *square)
+        idx = jnp.transpose(grid_idx, (1, 0)).reshape(3, *square)
+        msg = spread(w, idx, charge.reshape(square), real_mask.reshape(square), fh, fl)
         recv, ghost = exchange(msg)
         own, other = y_transform(recv, ghost, ch, cl)
         mode_energy, energy = z_transform(own, other, ch, cl, influence)

time: 178 us -> 167 us (0.938); the launches traced: 178 us -> 165 us
  Pallas kernels: 173 us -> 156 us
  local copies, waits for them, and re-layouts: 3 us -> 7.19 us
    pallas_call x1, Pallas kernels: 94.4 us -> 77.7 us  [spread(): pl.pallas_call(spread_kernel, out_shape=jax.ShapeDtypeStruct((NY, BLOCK,...]
    pallas_call x1, Pallas kernels: 56.7 us -> 54.1 us  [exchange(): pl.pallas_call(exchange_kernel, out_shape=(jax.ShapeDtypeStruct((NY, BLOC...]
    reshape x0 -> x1, local copies, waits for them, and re-layouts: none -> 2.55 us  [local_energy(): w = jnp.transpose(spline_w, (1, 2, 0)).reshape(3 * TAPS, *square)]
    unnamed x9 -> x10, local copies, waits for them, and re-layouts: 3 us -> 4.64 us
where the time goes in v3:
time: 167 us; the launch traced here: 165 us
  Pallas kernels  156 us (93%)
  local copies, waits for them, and re-layouts  7.19 us (4%)
  between operations  1.85 us (1%)
    pallas_call x1, Pallas kernels, spread(): pl.pallas_call(spread_kernel, out_shape=jax.ShapeDtypeStruct((NY, BLOCK,...  77.7 us
    pallas_call x1, Pallas kernels, exchange(): pl.pallas_call(exchange_kernel, out_shape=(jax.ShapeDtypeStruct((NY, BLOC...  54.1 us
    pallas_call x1, Pallas kernels, z_transform(): pl.pallas_call(z_kernel, out_shape=(jax.ShapeDtypeStruct((6, LEN_Z, G), F...  13.8 us
    pallas_call x1, Pallas kernels, y_transform(): pl.pallas_call(y_kernel, out_shape=(half, half), in_specs=[pl.BlockSpec(m...  10.7 us
    unnamed x10, local copies, waits for them, and re-layouts  4.64 us

profile of v3, /device:TPU:1, one launch (start us, length us, event | category | flops | bytes accessed | tf_op | source)
XLA Modules:
  0.0 165.3 jit_solution(17844265495677401680)
XLA Ops:
  0.6 1.6 copy.13
  2.3 2.6 %reshape.16.w_ref = f32[12,128,128]{2,1,0:T(8,128)} reshape(f32[3,4,16384]{2,1,0:T(4,128)} %bitcast.12) | data formatting | bytes 1572864 | tf_op jit(solution)/shard_map/reshape | solution.py:563
  4.8 77.7 %spread.1.msg_ref = s16[64,168,128]{2,1,0:T(8,128)(2,1)} custom-call(f32[12,128,128]{2,1,0:T(8,128)} %reshape.16.w_ref, s32[3,128,128]{2,1,0:T(8,128)} %bitcast.11, f32[128,128]{1,0:T(8,128)} %bitcast.14, s32[128,128]{1,0:T(8,128)} %bitcast.15, bf16[768,384]{1,0:T(8,128)(2,1)} %constant.8.clone.fh_ref, bf16[768,384]{1,0:T(8,128)(2,1)} %constant.9.clone.fl_ref), custom_call_target="tpu_custom_call" | custom-call | tf_op jit(solution)/shard_map/spread/pallas_call | solution.py:224
  82.6 0.0 copy-start
  82.6 1.8 %copy-done = s16[64,168,128]{2,1,0:T(8,128)(2,1)S(1)} copy-done((s16[64,168,128]{2,1,0:T(8,128)(2,1)S(1)}, s16[64,168,128]{2,1,0:T(8,128)(2,1)}, u32[]{:S(2)}) %copy-start) | copy-done | bytes 2752536
  84.3 0.0 copy-start.1
  84.3 0.0 copy-start.2
  84.3 54.1 %exchange.1 = (s16[64,168,128]{2,1,0:T(8,128)(2,1)S(1)}, s16[64,16,128]{2,1,0:T(8,128)(2,1)S(1)}) custom-call(s16[64,168,128]{2,1,0:T(8,128)(2,1)S(1)} %copy-done), custom_call_target="tpu_custom_call" | custom-call | tf_op jit(solution)/shard_map/exchange/pallas_call | solution.py:307
  138.5 0.0 copy-done.1
  138.5 0.0 copy-done.2
  138.5 0.0 copy-start.3
  138.5 10.7 %y_transform.1 = (f32[3,192,768]{2,1,0:T(8,128)S(1)}, f32[3,192,768]{2,1,0:T(8,128)S(1)}) custom-call(s16[64,168,128]{2,1,0:T(8,128)(2,1)S(1)} %get-tuple-element.8.recv16_ref, s16[64,16,128]{2,1,0:T(8,128)(2,1)S(1)} %get-tuple-element.9.ghost16_ref, bf16[384,768]{1,0:T(8,128)(2,1)S(1)} %copy-done.2, bf16[384,768]{1,0:T(8,128)(2,1)S(1)} %copy-done.1), custom_call_target="tpu_custom_call" | custom-call | tf_op jit(solution)/shard_map/y_transform/pallas_call | solution.py:420
  149.2 0.0 copy-done.3
  149.2 13.8 %z_transform.1 = (f32[6,192,384]{2,1,0:T(8,128)S(1)}, f32[1,128]{1,0:T(1,128)S(1)}) custom-call(f32[3,192,768]{2,1,0:T(8,128)S(1)} %get-tuple-element.10.own_ref, f32[3,192,768]{2,1,0:T(8,128)S(1)} %get-tuple-element.11.other_ref, bf16[384,768]{1,0:T(8,128)(2,1)S(1)} %copy-done.2, bf16[384,768]{1,0:T(8,128)(2,1)S(1)} %copy-done.1, f32[6,192,384]{2,1,0:T(8,128)S(1)} %copy-done.3), custom_call_target="tpu_custom_call" | custom-call | tf_op jit(solution)/shard_map/z_transform/pallas_call | solution.py:535
  162.9 1.2 copy.16
Async XLA Ops:
  82.6 1.8 %copy-start = (s16[64,168,128]{2,1,0:T(8,128)(2,1)S(1)}, s16[64,168,128]{2,1,0:T(8,128)(2,1)}, u32[]{:S(2)}) copy-start(s16[64,168,128]{2,1,0:T(8,128)(2,1)} %spread.1.msg_ref) | copy-start | bytes 8257540
  84.3 54.1 %copy-start.1 = (bf16[384,768]{1,0:T(8,128)(2,1)S(1)}, bf16[384,768]{1,0:T(8,128)(2,1)}, u32[]{:S(2)}) copy-start(bf16[384,768]{1,0:T(8,128)(2,1)} %constant.11.clone.cl_ref) | copy-start | bytes 1769476
  84.3 54.1 %copy-start.2 = (bf16[384,768]{1,0:T(8,128)(2,1)S(1)}, bf16[384,768]{1,0:T(8,128)(2,1)}, u32[]{:S(2)}) copy-start(bf16[384,768]{1,0:T(8,128)(2,1)} %constant.10.clone.ch_ref) | copy-start | bytes 1769476
  138.5 10.7 %copy-start.3 = (f32[6,192,384]{2,1,0:T(8,128)S(1)}, f32[6,192,384]{2,1,0:T(8,128)}, u32[]{:S(2)}) copy-start(f32[6,192,384]{2,1,0:T(8,128)} %bc_ref.1) | copy-start | bytes 5308420

commit v4 on v3

--- a/solution.py
+++ b/solution.py
@@ -14,8 +14,8 @@
 LEN_Z = 192
 EXT_Y = 9
 CHUNK = 256
-WINDOW = 128
-X_ROWS = 520
+WINDOW = 48
+X_ROWS = 440
 LANES = 128
 TILES = 14
 COLS = TILES * LANES
@@ -75,40 +75,88 @@
     return line
 
 
-def sort_lanes(key):
-    lane = lax.broadcasted_iota(jnp.int32, key.shape, 1)
+def sort_rows(keys):
+    lane = lax.broadcasted_iota(jnp.int32, keys[0].shape, 1)
+    keys = list(keys)
     size = 2
-    while size <= LANES:
+    while size <= LANES * len(keys):
         distance = size // 2
+        while distance >= LANES:
+            apart = distance // LANES
+            for v in range(len(keys)):
+                if not v & apart:
+                    a, b = keys[v], keys[v + apart]
+                    low, high = jnp.minimum(a, b), jnp.maximum(a, b)
+                    up = not v & (size // LANES)
+                    keys[v], keys[v + apart] = (low, high) if up else (high, low)
+            distance //= 2
         while distance:
             lower = lax.bitwise_and(lane, distance) == 0
-            other = jnp.where(lower, pltpu.roll(key, LANES - distance, 1), pltpu.roll(key, distance, 1))
-            ascending = lax.bitwise_and(lane, size) == 0
-            key = jnp.where(lower == ascending, jnp.minimum(key, other), jnp.maximum(key, other))
+            for v, key in enumerate(keys):
+                other = jnp.where(lower, pltpu.roll(key, LANES - distance, 1), pltpu.roll(key, distance, 1))
+                low, high = jnp.minimum(key, other), jnp.maximum(key, other)
+                if size < LANES:
+                    keys[v] = jnp.where(lower == (lax.bitwise_and(lane, size) == 0), low, high)
+                elif v & (size // LANES):
+                    keys[v] = jnp.where(lower, high, low)
+                else:
+                    keys[v] = jnp.where(lower, low, high)
             distance //= 2
         size *= 2
-    return key
+    return keys
 
 
 def spread_kernel(
     w_ref, idx_ref, q_ref, m_ref, fh_ref, fl_ref, msg_ref,
-    acc_ref, lz_ref, qh_ref, ql_ref, modes_ref, rows_ref, wgt_ref, base_ref, spare_ref, *bufs,
+    acc_ref, xl_ref, yl_ref, qh_ref, ql_ref, modes_ref, rows_ref, raw_ref, raw_base_ref, wgt_ref, base_ref, key_ref, *bufs,
 ):
-    lane = lax.broadcasted_iota(jnp.int32, (LANES, LANES), 1)
-    key = sort_lanes((idx_ref[0] * LANES + lane).astype(F32)).astype(jnp.int32)
-    order = lax.bitwise_and(key, LANES - 1)
-
-    def place(value):
-        return jnp.transpose(jnp.take_along_axis(value, order, axis=1))
-
-    base_ref[0] = jnp.transpose(lax.shift_right_logical(key, 7))
-    base_ref[1] = place(idx_ref[1])
-    base_ref[2] = place(idx_ref[2])
-    charge = q_ref[...] * m_ref[...].astype(F32)
-    for dim in range(3):
+    groups = LANES // 8
+
+    def unstack(block, carry):
+        for k in range(8):
+            row = 8 * block + k
+            span = pl.ds(pl.multiple_of(row * LANES, LANES), LANES)
+            for dim in range(3):
+                raw_base_ref[dim, pl.ds(row, 1), :] = idx_ref[dim : dim + 1, span]
+                for s in range(TAPS):
+                    raw_ref[TAPS * dim + s, pl.ds(row, 1), :] = w_ref[dim, s : s + 1, span]
+        return carry
+
+    lax.fori_loop(0, groups, unstack, 0)
+    lane = lax.broadcasted_iota(jnp.int32, (8, LANES), 1)
+    keys = []
+    for v in range(groups):
+        rows = slice(8 * v, 8 * v + 8)
+        keys.append((raw_base_ref[0, rows, :] * (LANES * groups) + (lane + LANES * v)).astype(F32))
+        raw_base_ref[1, rows, :] = raw_base_ref[1, rows, :] * 256 + raw_base_ref[2, rows, :]
+        charge = q_ref[rows, :] * m_ref[rows, :].astype(F32)
         for s in range(TAPS):
-            value = w_ref[TAPS * dim + s]
-            wgt_ref[TAPS * dim + s] = place(value * charge if dim == 0 else value)
+            raw_ref[s, rows, :] = raw_ref[s, rows, :] * charge
+    for v, key in enumerate(sort_rows(keys)):
+        key_ref[8 * v : 8 * v + 8, :] = key.astype(jnp.int32)
+
+    def permute(v, carry):
+        rows = pl.ds(pl.multiple_of(8 * v, 8), 8)
+        key = key_ref[rows, :]
+        base_ref[0, rows, :] = lax.shift_right_logical(key, 11)
+        vector = lax.bitwise_and(lax.shift_right_logical(key, 7), groups - 1)
+        source = lax.bitwise_and(key, LANES - 1)
+        hits = [vector == k for k in range(groups)]
+
+        def place(ref, field):
+            value = jnp.take_along_axis(ref[field, 0:8, :], source, axis=1)
+            for k in range(1, groups):
+                value = jnp.where(hits[k], jnp.take_along_axis(ref[field, 8 * k : 8 * k + 8, :], source, axis=1), value)
+            return value
+
+        both = place(raw_base_ref, 1)
+        base_ref[1, rows, :] = lax.shift_right_logical(both, 8)
+        base_ref[2, rows, :] = lax.bitwise_and(both, 255)
+        for field in range(3 * TAPS):
+            wgt_ref[field, rows, :] = place(raw_ref, field)
+        return carry
+
+    lax.fori_loop(0, groups, permute, 0)
 
     def row_of(ref, field, step):
         pieces = [
@@ -120,81 +168,94 @@
         base = row_of(base_ref, dim, step) - first
         return [base + s for s in range(TAPS)], [row_of(wgt_ref, TAPS * dim + s, step) for s in range(TAPS)]
 
-    def build_x(step, first, a):
+    def x_line(step, first):
         pos_x, wgt_x = taps(0, step, first)
         for g in range(WINDOW // 16):
-            high, low = split(pick(row_iota(16 * g, 16), pos_x, wgt_x))
-            a[16 * g : 16 * g + 16, :] = high
-            a[WINDOW + 16 * g : WINDOW + 16 * g + 16, :] = low
-
-    def build(step, a, bh, bl):
+            xl_ref[16 * g : 16 * g + 16, :] = pick(row_iota(16 * g, 16), pos_x, wgt_x)
+
+    def build_head(step, ah, al, zh, zl):
         bases = base_ref[0, pl.ds(2 * step, 2), :]
         first = jnp.min(bases) // 8 * 8
         windows = (jnp.max(bases) + 3 - first) // WINDOW + 1
-        build_x(step, first, a)
+        x_line(step, first)
+        pos_y, wgt_y = taps(1, step, 0)
+        yl_ref[...] = pick(row_iota(0, 16), pos_y, wgt_y)
         pos_z, wgt_z = taps(2, step, 0)
-        for g in range(LEN_Z // 16):
-            lz_ref[16 * g : 16 * g + 16, :] = pick(row_iota(16 * g, 16), pos_z, wgt_z)
-        pos_y, wgt_y = taps(1, step, 0)
-        for g in range(4):
-            rows = row_iota(16 * g, 16)
-            value = pick(lax.shift_right_logical(rows, 2), pos_y, wgt_y) * pick(
-                LEN_Z + lax.bitwise_and(rows, 3), pos_z, wgt_z
-            )
-            high, low = split(value)
-            bh[64 + 16 * g : 80 + 16 * g, :] = high
-            bl[64 + 16 * g : 80 + 16 * g, :] = low
-        for y in range(EXT_Y):
-            line = pick(jnp.full((16, CHUNK), y, jnp.int32), pos_y, wgt_y)
-            for g in range(LEN_Z // 16):
-                if g < 8:
-                    row = LANES * (LOW_TILE + y) + 16 * g
-                elif y == 8:
-                    row = 16 * (g - 8)
-                else:
-                    row = LANES * HIGH_TILE + 64 * y + 16 * (g - 8)
-                high, low = split(lz_ref[16 * g : 16 * g + 16, :] * line)
-                bh[row : row + 16, :] = high
-                bl[row : row + 16, :] = low
+        for g in range(LEN_Z // 16 + 1):
+            rows = slice(16 * g, 16 * g + 16)
+            zh[rows, :], zl[rows, :] = split(pick(row_iota(16 * g, 16), pos_z, wgt_z))
         return first, windows
 
-    def accumulate(first, a, bh, bl):
+    def build_group(step, group, ah, al):
+        for y in range(3 * group, 3 * group + 3):
+            line = jnp.broadcast_to(yl_ref[y : y + 1, :], (16, CHUNK))
+            for g in range(WINDOW // 16):
+                rows = slice(WINDOW * y + 16 * g, WINDOW * y + 16 * g + 16)
+                ah[rows, :], al[rows, :] = split(xl_ref[16 * g : 16 * g + 16, :] * line)
+
+    def accumulate(first, group, ah, al, zh, zl):
         span = pl.ds(pl.multiple_of(first, 8), WINDOW)
-        for t in range(TILES // 2):
-            cols = slice(256 * t, 256 * t + 256)
-            both = dot_nt(a[...], bh[cols, :])
-            acc_ref[span, cols] += both[:WINDOW] + both[WINDOW:] + dot_nt(a[:WINDOW, :], bl[cols, :])
-
-    def remaining(step, first, windows, a, bh, bl):
+        rows = slice(3 * WINDOW * group, 3 * WINDOW * (group + 1))
+        part = dot_nt(ah[rows, :], zh[...]) + dot_nt(al[rows, :], zh[...]) + dot_nt(ah[rows, :], zl[...])
+        for k in range(3):
+            acc_ref[3 * group + k, span, :] += part[WINDOW * k : WINDOW * k + WINDOW]
+
+    def stage(step, first, current, following):
+        ahead = build_head(step, *following)
+        for group in range(3):
+            accumulate(first, group, *current)
+            build_group(step, group, *following[:2])
+        return ahead
+
+    def remaining(step, first, windows, ah, al, zh, zl):
         def window(k, carry):
-            build_x(step, first + WINDOW * k, spare_ref)
-            accumulate(first + WINDOW * k, spare_ref, bh, bl)
+            x_line(step, first + WINDOW * k)
+            pos_y, wgt_y = taps(1, step, 0)
+            yl_ref[...] = pick(row_iota(0, 16), pos_y, wgt_y)
+            for group in range(3):
+                build_group(step, group, ah, al)
+                accumulate(first + WINDOW * k, group, ah, al, zh, zl)
             return carry
 
         lax.fori_loop(1, windows, window, 0)
 
-    one, two = bufs[:3], bufs[3:]
+    one, two = bufs[:4], bufs[4:]
     acc_ref[...] = jnp.zeros_like(acc_ref)
+    for buf in (one[2], one[3], two[2], two[3]):
+        buf[...] = jnp.zeros_like(buf)
     chunks = LANES * LANES // CHUNK
 
     def body(pair, carry):
         first, windows = carry
-        accumulate(first, *one)
-        next_first, next_windows = build(2 * pair + 1, *two)
+        ahead = stage(2 * pair + 1, first, one, two)
         remaining(2 * pair, first, windows, *one)
-        accumulate(next_first, *two)
-        carry = build(jnp.minimum(2 * pair + 2, chunks - 1), *one)
-        remaining(2 * pair + 1, next_first, next_windows, *two)
-        return carry
-
-    lax.fori_loop(0, chunks // 2, body, build(0, *one))
-    acc_ref[0:8, :] += acc_ref[G : G + 8, :]
-
-    for t in range(TILES // 2):
-        cols = slice(256 * t, 256 * t + 256)
-        high, low = split(acc_ref[:G, cols])
-        qh_ref[:, cols] = high
-        ql_ref[:, cols] = low
+        last = stage(jnp.minimum(2 * pair + 2, chunks - 1), ahead[0], two, one)
+        remaining(2 * pair + 1, *ahead, *two)
+        return last
+
+    start = build_head(0, *one)
+    for group in range(3):
+        build_group(0, group, *one[:2])
+    lax.fori_loop(0, chunks // 2, body, start)
+
+    lane = lax.broadcasted_iota(jnp.int32, (G, LANES), 1)
+
+    def put(t, value):
+        cols = slice(LANES * t, LANES * t + LANES)
+        qh_ref[:, cols], ql_ref[:, cols] = split(value)
+
+    for y in range(EXT_Y):
+        acc_ref[y, 0:8, :] += acc_ref[y, G : G + 8, :]
+        put(LOW_TILE + y, acc_ref[y, :G, :LANES])
+        high = acc_ref[y, :G, LANES:]
+        ghost = jnp.where(lane < 64, 0.0, high)
+        ghosts = ghost if y == 0 else ghosts + pltpu.roll(ghost, 4 * y, 1)
+        if y == 8:
+            put(0, jnp.where(lane < 64, high, ghosts))
+        elif y % 2:
+            put(HIGH_TILE + y // 2, jnp.where(lane < 64, even, pltpu.roll(high, 64, 1)))
+        else:
+            even = high
     for t in range(TILES // 2):
         cols = slice(256 * t, 256 * t + 256)
         part = dot(fh_ref[...], qh_ref[:, cols]) + dot(fl_ref[...], qh_ref[:, cols]) + dot(fh_ref[...], ql_ref[:, cols])
@@ -227,8 +288,9 @@
         in_specs=[pl.BlockSpec(memory_space=pltpu.VMEM)] * 6,
         out_specs=pl.BlockSpec(memory_space=pltpu.VMEM),
         scratch_shapes=[
-            pltpu.VMEM((X_ROWS, COLS), F32),
-            pltpu.VMEM((LEN_Z, CHUNK), F32),
+            pltpu.VMEM((EXT_Y, X_ROWS, 2 * LANES), F32),
+            pltpu.VMEM((WINDOW, CHUNK), F32),
+            pltpu.VMEM((16, CHUNK), F32),
             pltpu.VMEM((G, COLS), BF),
             pltpu.VMEM((G, COLS), BF),
             pltpu.VMEM((ROWS * NY, COLS), F32),
@@ -237,12 +299,15 @@
         + [
             pltpu.VMEM((3 * TAPS, LANES, LANES), F32),
             pltpu.VMEM((3, LANES, LANES), jnp.int32),
-            pltpu.VMEM((2 * WINDOW, CHUNK), BF),
+            pltpu.VMEM((3 * TAPS, LANES, LANES), F32),
+            pltpu.VMEM((3, LANES, LANES), jnp.int32),
+            pltpu.VMEM((LANES, LANES), jnp.int32),
         ]
         + [
-            pltpu.VMEM((2 * WINDOW, CHUNK), BF),
-            pltpu.VMEM((COLS, CHUNK), BF),
-            pltpu.VMEM((COLS, CHUNK), BF),
+            pltpu.VMEM((EXT_Y * WINDOW, CHUNK), BF),
+            pltpu.VMEM((EXT_Y * WINDOW, CHUNK), BF),
+            pltpu.VMEM((2 * LANES, CHUNK), BF),
+            pltpu.VMEM((2 * LANES, CHUNK), BF),
         ]
         * 2,
         compiler_params=pltpu.CompilerParams(vmem_limit_bytes=60 * 1024 * 1024),
@@ -560,8 +625,8 @@
     def local_energy(charge, real_mask, grid_idx, spline_w, influence):
         fh, fl, ch, cl = [jnp.asarray(table) for table in tables]
         square = (LANES, LANES)
-        w = jnp.transpose(spline_w, (1, 2, 0)).reshape(3 * TAPS, *square)
-        idx = jnp.transpose(grid_idx, (1, 0)).reshape(3, *square)
+        w = jnp.transpose(spline_w, (1, 2, 0))
+        idx = jnp.transpose(grid_idx, (1, 0))
         msg = spread(w, idx, charge.reshape(square), real_mask.reshape(square), fh, fl)
         recv, ghost = exchange(msg)
         own, other = y_transform(recv, ghost, ch, cl)

time: 167 us -> 141 us (0.84)
  Pallas kernels: 156 us -> 136 us
  local copies, waits for them, and re-layouts: 7.19 us -> 3 us
    pallas_call x1, Pallas kernels: 77.7 us -> 56.4 us  [spread(): pl.pallas_call(spread_kernel, out_shape=jax.ShapeDtypeStruct((NY, BLOCK,...]
    reshape x1 -> x0, local copies, waits for them, and re-layouts: 2.55 us -> none  [local_energy(): w = jnp.transpose(spline_w, (1, 2, 0)).reshape(3 * TAPS, *square)]
    pallas_call x1, Pallas kernels: 54.1 us -> 56.4 us  [exchange(): pl.pallas_call(exchange_kernel, out_shape=(jax.ShapeDtypeStruct((NY, BLOC...]
    unnamed x10 -> x9, local copies, waits for them, and re-layouts: 4.64 us -> 3 us
where the time goes in v4:
time: 141 us
  Pallas kernels  136 us (96%)
  local copies, waits for them, and re-layouts  3 us (2%)
  between operations  1.85 us (1%)
    pallas_call x1, Pallas kernels, exchange(): pl.pallas_call(exchange_kernel, out_shape=(jax.ShapeDtypeStruct((NY, BLOC...  56.4 us
    pallas_call x1, Pallas kernels, spread(): pl.pallas_call(spread_kernel, out_shape=jax.ShapeDtypeStruct((NY, BLOCK,...  56.4 us
    pallas_call x1, Pallas kernels, z_transform(): pl.pallas_call(z_kernel, out_shape=(jax.ShapeDtypeStruct((6, LEN_Z, G), F...  12.3 us
    pallas_call x1, Pallas kernels, y_transform(): pl.pallas_call(y_kernel, out_shape=(half, half), in_specs=[pl.BlockSpec(m...  10.6 us
    unnamed x9, local copies, waits for them, and re-layouts  3 us

profile of v4, /device:TPU:1, one launch (start us, length us, event | category | flops | bytes accessed | tf_op | source)
XLA Modules:
  0.0 140.7 jit_solution(11650888335356991101)
XLA Ops:
  0.6 56.4 %spread.1.msg_ref = s16[64,168,128]{2,1,0:T(8,128)(2,1)} custom-call(f32[3,4,16384]{2,1,0:T(4,128)} %bitcast.7, s32[3,16384]{1,0:T(4,128)} %bitcast.8, f32[128,128]{1,0:T(8,128)} %bitcast.9, s32[128,128]{1,0:T(8,128)} %bitcast.10, bf16[768,384]{1,0:T(8,128)(2,1)} %constant.8.clone.fh_ref, bf16[768,384]{1,0:T(8,128)(2,1)} %constant.9.clone.fl_ref), custom_call_target="tpu_custom_call" | custom-call | tf_op jit(solution)/shard_map/spread/pallas_call | solution.py:285
  57.1 0.0 copy-start
  57.1 1.8 %copy-done = s16[64,168,128]{2,1,0:T(8,128)(2,1)S(1)} copy-done((s16[64,168,128]{2,1,0:T(8,128)(2,1)S(1)}, s16[64,168,128]{2,1,0:T(8,128)(2,1)}, u32[]{:S(2)}) %copy-start) | copy-done | bytes 2752536
  58.8 0.0 copy-start.1
  58.8 0.0 copy-start.2
  58.8 56.4 %exchange.1 = (s16[64,168,128]{2,1,0:T(8,128)(2,1)S(1)}, s16[64,16,128]{2,1,0:T(8,128)(2,1)S(1)}) custom-call(s16[64,168,128]{2,1,0:T(8,128)(2,1)S(1)} %copy-done), custom_call_target="tpu_custom_call" | custom-call | tf_op jit(solution)/shard_map/exchange/pallas_call | solution.py:372
  115.3 0.0 copy-done.1
  115.3 0.0 copy-done.2
  115.3 0.0 copy-start.3
  115.3 10.6 %y_transform.1 = (f32[3,192,768]{2,1,0:T(8,128)S(1)}, f32[3,192,768]{2,1,0:T(8,128)S(1)}) custom-call(s16[64,168,128]{2,1,0:T(8,128)(2,1)S(1)} %get-tuple-element.8.recv16_ref, s16[64,16,128]{2,1,0:T(8,128)(2,1)S(1)} %get-tuple-element.9.ghost16_ref, bf16[384,768]{1,0:T(8,128)(2,1)S(1)} %copy-done.2, bf16[384,768]{1,0:T(8,128)(2,1)S(1)} %copy-done.1), custom_call_target="tpu_custom_call" | custom-call | tf_op jit(solution)/shard_map/y_transform/pallas_call | solution.py:485
  126.0 0.0 copy-done.3
  126.0 12.3 %z_transform.1 = (f32[6,192,384]{2,1,0:T(8,128)S(1)}, f32[1,128]{1,0:T(1,128)S(1)}) custom-call(f32[3,192,768]{2,1,0:T(8,128)S(1)} %get-tuple-element.10.own_ref, f32[3,192,768]{2,1,0:T(8,128)S(1)} %get-tuple-element.11.other_ref, bf16[384,768]{1,0:T(8,128)(2,1)S(1)} %copy-done.2, bf16[384,768]{1,0:T(8,128)(2,1)S(1)} %copy-done.1, f32[6,192,384]{2,1,0:T(8,128)S(1)} %copy-done.3), custom_call_target="tpu_custom_call" | custom-call | tf_op jit(solution)/shard_map/z_transform/pallas_call | solution.py:600
  138.3 1.2 copy.13
Async XLA Ops:
  57.1 1.8 %copy-start = (s16[64,168,128]{2,1,0:T(8,128)(2,1)S(1)}, s16[64,168,128]{2,1,0:T(8,128)(2,1)}, u32[]{:S(2)}) copy-start(s16[64,168,128]{2,1,0:T(8,128)(2,1)} %spread.1.msg_ref) | copy-start | bytes 8257540
  58.8 56.5 %copy-start.1 = (bf16[384,768]{1,0:T(8,128)(2,1)S(1)}, bf16[384,768]{1,0:T(8,128)(2,1)}, u32[]{:S(2)}) copy-start(bf16[384,768]{1,0:T(8,128)(2,1)} %constant.11.clone.cl_ref) | copy-start | bytes 1769476
  58.8 56.5 %copy-start.2 = (bf16[384,768]{1,0:T(8,128)(2,1)S(1)}, bf16[384,768]{1,0:T(8,128)(2,1)}, u32[]{:S(2)}) copy-start(bf16[384,768]{1,0:T(8,128)(2,1)} %constant.10.clone.ch_ref) | copy-start | bytes 1769476
  115.3 10.7 %copy-start.3 = (f32[6,192,384]{2,1,0:T(8,128)S(1)}, f32[6,192,384]{2,1,0:T(8,128)}, u32[]{:S(2)}) copy-start(f32[6,192,384]{2,1,0:T(8,128)} %bc_ref.1) | copy-start | bytes 5308420
